TPU v7x, 32 devices: a 4x4x1 block of a 4x4x8 slice. The times are simulated.
32 devices in a mesh: rhs: 1 (over z), mode1: 4 (over y), mode2: 4 (over x), mode3: 2 (over core).
Axes of the slice: x: 4, y: 4, z: 1, core: 2. Of those that a mesh axis runs over, the one named last changes fastest.
The devices are a block of a 4x4x8 slice.
Arguments:
- x_vol: bfloat16 [8, 128, 256, 512], P('rhs', 'mode1', 'mode2', 'mode3')
- diag_vals: float32 [128, 256, 512], P('mode1', 'mode2', 'mode3')
- a_mode1: bfloat16 [128, 128], replicated
- a_mode2: bfloat16 [256, 256], replicated
- a_mode3: bfloat16 [512, 512], replicated
- b_mode1: bfloat16 [128, 128], replicated
- b_mode2: bfloat16 [256, 256], replicated
- b_mode3: bfloat16 [512, 512], replicated
Outputs:
- output: float32 [8, 128, 256, 512], P('rhs', 'mode1', 'mode2', 'mode3')
All inputs are finite; a program needn't handle non-finite values.
Results may differ from a plain program's by a relative error of at most 0.010905.
Values are sent between devices in bfloat16 or wider.
A program may use at most 768 MiB of HBM per device.

v0:
```python
import jax
import jax.numpy as jnp
from jax import lax
from jax.sharding import PartitionSpec as P


def mode_sum(volume, mat_one, mat_two, mat_three):
    whole_one = lax.all_to_all(volume, 'mode1', 2, 1, tiled=True)
    part_one = jnp.einsum('ia,rajk->rijk', mat_one, whole_one, preferred_element_type=jnp.float32).astype(jnp.bfloat16)
    term_one = lax.all_to_all(part_one, 'mode1', 1, 2, tiled=True)
    whole_two = lax.all_to_all(volume, 'mode2', 1, 2, tiled=True)
    part_two = jnp.einsum('jb,ribk->rijk', mat_two, whole_two, preferred_element_type=jnp.float32).astype(jnp.bfloat16)
    term_two = lax.all_to_all(part_two, 'mode2', 2, 1, tiled=True)
    whole_three = lax.all_to_all(volume, 'mode3', 2, 3, tiled=True)
    part_three = jnp.einsum('rijc,kc->rijk', whole_three, mat_three, preferred_element_type=jnp.float32).astype(jnp.bfloat16)
    term_three = lax.all_to_all(part_three, 'mode3', 3, 2, tiled=True)
    return term_one.astype(jnp.float32) + term_two.astype(jnp.float32) + term_three.astype(jnp.float32)


def solution(mesh):
    vol_spec = P('rhs', 'mode1', 'mode2', 'mode3')
    diag_spec = P('mode1', 'mode2', 'mode3')

    def local_op(x_vol, diag_vals, a_mode1, a_mode2, a_mode3, b_mode1, b_mode2, b_mode3):
        u_vol = mode_sum(x_vol, a_mode1, a_mode2, a_mode3).astype(jnp.bfloat16)
        w_vol = (diag_vals * u_vol.astype(jnp.float32)).astype(jnp.bfloat16)
        return mode_sum(w_vol, b_mode1, b_mode2, b_mode3)

    return jax.shard_map(local_op, mesh=mesh, in_specs=(vol_spec, diag_spec, P(), P(), P(), P(), P(), P()), out_specs=vol_spec, check_vma=False)
```

profile of v0, /device:TPU:96, one launch (start us, length us, event | category | flops | bytes accessed | tf_op | source)
XLA Modules:
  0.0 1257.7 jit_solution(8313370881304845666)
XLA Ops:
  0.0 11.6 copy.125
  11.6 12.1 all_to_all.162
  23.7 20.4 %copy.185 = bf16[8,32,2,32,256]{4,2,3,1,0:T(2,128)(2,1)} copy(bf16[8,32,2,32,256]{4,1,0,3,2:T(8,128)(2,1)S(1)} %bitcast.128) | data formatting | bytes 16777216 | tf_op jit(solution)/shard_map/all_to_all | solution.py:14
  44.2 14.1 %all_to_all.133 = bf16[8,32,32,512]{3,2,1,0:T(8,128)(2,1)} reshape(bf16[8,32,32,2,256]{4,3,2,1,0:T(2,128)(2,1)} %bitcast.127) | data formatting | bytes 16777216 | tf_op jit(solution)/shard_map/all_to_all | solution.py:14
  58.2 10.2 convolution_convert_fusion.1
  68.5 44.3 %copy.141 = bf16[8,32,32,512]{2,1,0,3:T(8,128)(2,1)} copy(bf16[8,32,32,512]{3,2,1,0:T(8,128)(2,1)} %convolution_convert_fusion.1) | data formatting | bytes 16777216 | tf_op jit(solution)/shard_map/convert_element_type | solution.py:15
  112.8 27.6 %reshape.43 = bf16[2,2,1048576]{2,1,0:T(2,128)(2,1)} reshape(bf16[512,8,32,32]{3,2,1,0:T(8,128)(2,1)} %bitcast.112) | data formatting | bytes 16777216
  140.4 18.2 %all_to_all.163 = bf16[2,2,1048576]{2,1,0:T(2,128)(2,1)} all-to-all(bf16[2,2,1048576]{2,1,0:T(2,128)(2,1)} %reshape.43), channel_id=1, replica_groups=mesh['rhs'=1,'mode1'=4,'mode2'=4,'mode3'=2] {'mode3'}, dimensions={0} | all-to-all | bytes 16777216 | tf_op jit(solution)/shard_map/all_to_all | solution.py:16
  172.6 86.6 %all-to-all-done = bf16[8,32,64,256]{3,1,0,2:T(8,128)(2,1)} async-done(((bf16[8,32,64,256]{3,1,0,2:T(8,128)(2,1)}), bf16[8,32,64,256]{3,1,0,2:T(8,128)(2,1)}, u32[]{:S(2)}, u32[]{:S(2)}) %all-to-all-start) | async-done | bytes 8388640 | tf_op jit(solution)/shard_map/all_to_all | solution.py:8
  265.3 15.3 %copy.127 = bf16[8,4,32,16,256]{4,3,2,1,0:T(8,128)(2,1)} copy(bf16[8,4,32,16,256]{4,2,0,3,1:T(8,128)(2,1)} %bitcast.2) | data formatting | bytes 16777216 | tf_op jit(solution)/shard_map/all_to_all | solution.py:8
  280.6 15.8 %convert_bitcast_fusion.7 = bf16[8,128,16,256]{1,3,2,0:T(8,128)(2,1)} fusion(bf16[8,128,16,256]{3,2,1,0:T(8,128)(2,1)} %bitcast.119, bf16[128,128]{1,0:T(8,128)(2,1)S(1)} %copy-done.5), kind=kOutput, calls=%fused_computation.18 | convolution fusion | flops 1077936128 | bytes 16809984 | tf_op jit(solution)/shard_map/ia,rajk->rijk/dot_general | solution.py:9
  296.4 12.6 %copy.129 = bf16[8,128,16,256]{3,2,0,1:T(8,128)(2,1)} copy(bf16[8,128,16,256]{1,3,2,0:T(8,128)(2,1)} %convert_bitcast_fusion.7) | data formatting | bytes 16777216 | tf_op jit(solution)/shard_map/convert_element_type | solution.py:9
  309.0 49.6 %all-to-all-done.2 = bf16[8,32,64,256]{3,2,0,1:T(8,128)(2,1)} async-done(((bf16[8,32,64,256]{3,2,0,1:T(8,128)(2,1)}), bf16[8,32,64,256]{3,2,0,1:T(8,128)(2,1)}, u32[]{:S(2)}, u32[]{:S(2)}) %all-to-all-start.2) | async-done | bytes 8388640 | tf_op jit(solution)/shard_map/all_to_all | solution.py:11
  372.8 9.0 convert_bitcast_fusion.6
  381.8 12.2 copy.136
  394.0 62.8 %all-to-all-done.1 = bf16[8,128,16,256]{3,2,0,1:T(8,128)(2,1)} async-done(((bf16[8,128,16,256]{3,2,0,1:T(8,128)(2,1)}), bf16[8,128,16,256]{3,2,0,1:T(8,128)(2,1)}, u32[]{:S(2)}, u32[]{:S(2)}) %all-to-all-start.1) | async-done | bytes 8388640 | tf_op jit(solution)/shard_map/all_to_all | solution.py:10
  462.8 38.1 %reshape.44 = bf16[512,8,32,32]{3,2,1,0:T(8,128)(2,1)} reshape(bf16[2,2,1048576]{2,1,0:T(2,128)(2,1)} %all_to_all.163) | data formatting | bytes 16777216
  500.9 33.7 %copy.142 = bf16[8,32,32,512]{3,2,1,0:T(8,128)(2,1)} copy(bf16[8,32,32,512]{2,1,0,3:T(8,128)(2,1)} %bitcast.113) | data formatting | bytes 16777216 | tf_op jit(solution)/shard_map/all_to_all | solution.py:16
  534.6 18.0 %reshape.33 = f32[8,32,32,2,256]{4,3,2,1,0:T(2,128)} reshape(bf16[8,32,32,512]{3,2,1,0:T(8,128)(2,1)} %copy.142) | data formatting | bytes 25165824 | tf_op jit(solution)/shard_map/convert_element_type | solution.py:17
  552.6 12.7 %copy.143 = f32[8,32,2,32,256]{4,3,2,1,0:T(8,128)} copy(f32[8,32,2,32,256]{4,2,3,1,0:T(2,128)} %bitcast.116) | data formatting | bytes 33554432 | tf_op jit(solution)/shard_map/convert_element_type | solution.py:17
  572.7 11.8 convert_bitcast_fusion.3
  584.6 12.3 copy.131
  596.9 11.4 copy.137
  608.3 11.7 convert_bitcast_fusion.2
  627.0 15.6 %multiply_convert_fusion = bf16[8,32,64,256]{3,2,1,0:T(8,128)(2,1)} fusion(f32[8,32,2,32,256]{4,3,2,1,0:T(8,128)} %copy.143, f32[8,32,64,256]{3,2,1,0:T(8,128)S(1)} %bitcast.117, f32[8,32,4,16,256]{4,3,2,1,0:T(8,128)} %copy.131, f32[32,64,256]{2,1,0:T(8,128)S(1)} %copy-done.2), kind=kLoop, calls=%fused_computation.9 | loop fusion | flops 25165824 | bytes 60817408 | tf_op jit(solution)/shard_map/convert_element_type | solution.py:26
  642.6 11.4 copy.144
  654.0 12.1 all_to_all.164
  666.1 20.4 %copy.160 = bf16[8,32,32,2,256]{4,3,2,1,0:T(2,128)(2,1)} copy(bf16[8,32,32,2,256]{4,1,0,2,3:T(8,128)(2,1)S(1)} %bitcast.129) | data formatting | bytes 16777216 | tf_op jit(solution)/shard_map/all_to_all | solution.py:14
  686.5 14.1 %all_to_all.148 = bf16[8,32,32,512]{3,2,1,0:T(8,128)(2,1)} reshape(bf16[8,32,32,2,256]{4,3,2,1,0:T(2,128)(2,1)} %copy.160) | data formatting | bytes 16777216 | tf_op jit(solution)/shard_map/all_to_all | solution.py:14
  700.7 10.3 convolution_convert_fusion
  710.9 44.3 %copy.161 = bf16[8,32,32,512]{2,1,0,3:T(8,128)(2,1)} copy(bf16[8,32,32,512]{3,2,1,0:T(8,128)(2,1)} %convolution_convert_fusion) | data formatting | bytes 16777216 | tf_op jit(solution)/shard_map/convert_element_type | solution.py:15
  755.3 27.6 %reshape.45 = bf16[2,2,1048576]{2,1,0:T(2,128)(2,1)} reshape(bf16[512,8,32,32]{3,2,1,0:T(8,128)(2,1)} %bitcast.114) | data formatting | bytes 16777216
  782.9 18.2 %all_to_all.165 = bf16[2,2,1048576]{2,1,0:T(2,128)(2,1)} all-to-all(bf16[2,2,1048576]{2,1,0:T(2,128)(2,1)} %reshape.45), channel_id=1, replica_groups=mesh['rhs'=1,'mode1'=4,'mode2'=4,'mode3'=2] {'mode3'}, dimensions={0} | all-to-all | bytes 16777216 | tf_op jit(solution)/shard_map/all_to_all | solution.py:16
  815.1 86.0 %all-to-all-done.6 = bf16[8,32,64,256]{3,1,0,2:T(8,128)(2,1)} async-done(((bf16[8,32,64,256]{3,1,0,2:T(8,128)(2,1)}), bf16[8,32,64,256]{3,1,0,2:T(8,128)(2,1)}, u32[]{:S(2)}, u32[]{:S(2)}) %all-to-all-start.6) | async-done | bytes 8388640 | tf_op jit(solution)/shard_map/all_to_all | solution.py:8
  907.1 15.3 %copy.146 = bf16[8,4,32,16,256]{4,3,2,1,0:T(8,128)(2,1)} copy(bf16[8,4,32,16,256]{4,2,0,3,1:T(8,128)(2,1)} %bitcast.28) | data formatting | bytes 16777216 | tf_op jit(solution)/shard_map/all_to_all | solution.py:8
  922.4 15.8 %convert_bitcast_fusion.5 = bf16[8,128,16,256]{1,3,2,0:T(8,128)(2,1)} fusion(bf16[8,128,16,256]{3,2,1,0:T(8,128)(2,1)} %bitcast.120, bf16[128,128]{1,0:T(8,128)(2,1)S(1)} %copy-done.6), kind=kOutput, calls=%fused_computation.16 | convolution fusion | flops 1077936128 | bytes 16809984 | tf_op jit(solution)/shard_map/ia,rajk->rijk/dot_general | solution.py:9
  938.2 12.5 copy.148
  950.7 49.7 %all-to-all-done.8 = bf16[8,32,64,256]{3,2,0,1:T(8,128)(2,1)} async-done(((bf16[8,32,64,256]{3,2,0,1:T(8,128)(2,1)}), bf16[8,32,64,256]{3,2,0,1:T(8,128)(2,1)}, u32[]{:S(2)}, u32[]{:S(2)}) %all-to-all-start.8) | async-done | bytes 8388640 | tf_op jit(solution)/shard_map/all_to_all | solution.py:11
  1014.6 9.0 convert_bitcast_fusion.4
  1023.6 12.2 copy.155
  1035.8 62.8 %all-to-all-done.7 = bf16[8,128,16,256]{3,2,0,1:T(8,128)(2,1)} async-done(((bf16[8,128,16,256]{3,2,0,1:T(8,128)(2,1)}), bf16[8,128,16,256]{3,2,0,1:T(8,128)(2,1)}, u32[]{:S(2)}, u32[]{:S(2)}) %all-to-all-start.7) | async-done | bytes 8388640 | tf_op jit(solution)/shard_map/all_to_all | solution.py:10
  1104.6 38.1 %reshape.46 = bf16[512,8,32,32]{3,2,1,0:T(8,128)(2,1)} reshape(bf16[2,2,1048576]{2,1,0:T(2,128)(2,1)} %all_to_all.165) | data formatting | bytes 16777216
  1142.7 36.7 %copy.162 = f32[8,32,32,2,256]{4,2,3,1,0:T(8,128)} copy(bf16[8,32,32,2,256]{2,1,0,4,3:T(8,128)(2,1)} %bitcast.115) | data formatting | bytes 25165824 | tf_op jit(solution)/shard_map/convert_element_type | solution.py:17
  1186.8 11.8 convert_bitcast_fusion.1
  1198.7 12.1 copy.150
  1210.8 11.4 copy.156
  1222.2 11.7 convert_bitcast_fusion
  1240.4 17.1 %bitcast_add_fusion = f32[8,32,64,256]{3,2,1,0:T(8,128)} fusion(f32[8,32,32,2,256]{4,2,3,1,0:T(8,128)} %copy.162, f32[8,32,64,256]{3,2,1,0:T(8,128)S(1)} %bitcast.118, f32[8,32,4,16,256]{4,3,2,1,0:T(8,128)} %copy.150), kind=kLoop, calls=%fused_computation | loop fusion | flops 8388608 | bytes 67108864 | tf_op jit(solution)/shard_map/add | solution.py:17
  (34 shorter events, 108.6 us)
Async XLA Ops:
  0.0 58.2 %copy-start = (bf16[512,512]{1,0:T(8,128)(2,1)S(1)}, bf16[512,512]{1,0:T(8,128)(2,1)}, u32[]{:S(2)}) copy-start(bf16[512,512]{1,0:T(8,128)(2,1)} %param.12) | copy-start | bytes 1572868
  158.6 100.6 %all-to-all-start = ((bf16[8,32,64,256]{3,1,0,2:T(8,128)(2,1)}), bf16[8,32,64,256]{3,1,0,2:T(8,128)(2,1)}, u32[]{:S(2)}, u32[]{:S(2)}) async-start(bf16[8,32,64,256]{3,1,0,2:T(8,128)(2,1)} %copy.125), calls=%async_computation | async-start | bytes 16777216 | tf_op jit(solution)/shard_map/all_to_all | solution.py:8
  259.3 99.3 %all-to-all-start.2 = ((bf16[8,32,64,256]{3,2,0,1:T(8,128)(2,1)}), bf16[8,32,64,256]{3,2,0,1:T(8,128)(2,1)}, u32[]{:S(2)}, u32[]{:S(2)}) async-start(bf16[8,32,64,256]{3,2,0,1:T(8,128)(2,1)} %copy.132), calls=%async_computation.2 | async-start | bytes 16777216 | tf_op jit(solution)/shard_map/all_to_all | solution.py:11
  265.3 15.3 %copy-start.5 = (bf16[128,128]{1,0:T(8,128)(2,1)S(1)}, bf16[128,128]{1,0:T(8,128)(2,1)}, u32[]{:S(2)}) copy-start(bf16[128,128]{1,0:T(8,128)(2,1)} %param.10) | copy-start | bytes 98308
  358.6 98.3 %all-to-all-start.1 = ((bf16[8,128,16,256]{3,2,0,1:T(8,128)(2,1)}), bf16[8,128,16,256]{3,2,0,1:T(8,128)(2,1)}, u32[]{:S(2)}, u32[]{:S(2)}) async-start(bf16[8,128,16,256]{3,2,0,1:T(8,128)(2,1)} %copy.129), calls=%async_computation.1 | async-start | bytes 16777216 | tf_op jit(solution)/shard_map/all_to_all | solution.py:10
  364.3 8.5 copy-start.3
  456.8 140.1 %all-to-all-start.3 = ((bf16[8,8,256,256]{3,1,0,2:T(8,128)(2,1)}), bf16[8,8,256,256]{3,1,0,2:T(8,128)(2,1)}, u32[]{:S(2)}, u32[]{:S(2)}) async-start(bf16[8,8,256,256]{3,1,0,2:T(8,128)(2,1)} %copy.136), calls=%async_computation.3 | async-start | bytes 16777216 | tf_op jit(solution)/shard_map/all_to_all | solution.py:13
  620.0 7.0 copy-start.2
  686.5 14.1 %copy-start.7 = (bf16[512,512]{1,0:T(8,128)(2,1)S(1)}, bf16[512,512]{1,0:T(8,128)(2,1)}, u32[]{:S(2)}) copy-start(bf16[512,512]{1,0:T(8,128)(2,1)} %param.15) | copy-start | bytes 1572868
  801.1 100.0 %all-to-all-start.6 = ((bf16[8,32,64,256]{3,1,0,2:T(8,128)(2,1)}), bf16[8,32,64,256]{3,1,0,2:T(8,128)(2,1)}, u32[]{:S(2)}, u32[]{:S(2)}) async-start(bf16[8,32,64,256]{3,1,0,2:T(8,128)(2,1)} %copy.144), calls=%async_computation.6 | async-start | bytes 16777216 | tf_op jit(solution)/shard_map/all_to_all | solution.py:8
  901.1 99.3 %all-to-all-start.8 = ((bf16[8,32,64,256]{3,2,0,1:T(8,128)(2,1)}), bf16[8,32,64,256]{3,2,0,1:T(8,128)(2,1)}, u32[]{:S(2)}, u32[]{:S(2)}) async-start(bf16[8,32,64,256]{3,2,0,1:T(8,128)(2,1)} %copy.151), calls=%async_computation.8 | async-start | bytes 16777216 | tf_op jit(solution)/shard_map/all_to_all | solution.py:11
  907.0 15.3 %copy-start.6 = (bf16[128,128]{1,0:T(8,128)(2,1)S(1)}, bf16[128,128]{1,0:T(8,128)(2,1)}, u32[]{:S(2)}) copy-start(bf16[128,128]{1,0:T(8,128)(2,1)} %param.13) | copy-start | bytes 98308
  1000.4 98.3 %all-to-all-start.7 = ((bf16[8,128,16,256]{3,2,0,1:T(8,128)(2,1)}), bf16[8,128,16,256]{3,2,0,1:T(8,128)(2,1)}, u32[]{:S(2)}, u32[]{:S(2)}) async-start(bf16[8,128,16,256]{3,2,0,1:T(8,128)(2,1)} %copy.148), calls=%async_computation.7 | async-start | bytes 16777216 | tf_op jit(solution)/shard_map/all_to_all | solution.py:10
  1006.1 8.5 copy-start.4
  1098.7 112.1 %all-to-all-start.9 = ((bf16[8,8,256,256]{3,1,0,2:T(8,128)(2,1)}), bf16[8,8,256,256]{3,1,0,2:T(8,128)(2,1)}, u32[]{:S(2)}, u32[]{:S(2)}) async-start(bf16[8,8,256,256]{3,1,0,2:T(8,128)(2,1)} %copy.155), calls=%async_computation.9 | async-start | bytes 16777216 | tf_op jit(solution)/shard_map/all_to_all | solution.py:13
  1240.4 17.1 %copy-start.1 = (bf16[512,512]{1,0:T(8,128)(2,1)S(1)}, bf16[512,512]{1,0:T(8,128)(2,1)}, u32[]{:S(2)}) copy-start(bf16[512,512]{1,0:T(8,128)(2,1)} %param.12) | copy-start | bytes 1572868
where the time goes:
time: 1270 us; the launch traced here: 1260 us
  local copies, waits for them, and re-layouts  603 us (47%)
  waiting for transfers between devices  398 us (31%)
  other arithmetic  79.8 us (6%)
  matrix products  70.1 us (6%)
  blocking collectives  60.7 us (5%)
  starting transfers between devices  46.6 us (4%)
    all_to_all x2, waiting for transfers between devices, mode_sum(): whole_one = lax.all_to_all(volume, 'mode1', 2, 1, tiled=True)  173 us
    unnamed x22, local copies, waits for them, and re-layouts  151 us
    all_to_all x2, waiting for transfers between devices, mode_sum(): term_one = lax.all_to_all(part_one, 'mode1', 1, 2, tiled=True)  126 us
    all_to_all x2, waiting for transfers between devices, mode_sum(): whole_two = lax.all_to_all(volume, 'mode2', 1, 2, tiled=True)  99.3 us
    convert_element_type x2, local copies, waits for them, and re-layouts, mode_sum(): jnp.einsum('rijc,kc->rijk', whole_three, mat_three, preferred_element_typ...  88.6 us
    all_to_all x4, local copies, waits for them, and re-layouts, mode_sum(): whole_three = lax.all_to_all(volume, 'mode3', 2, 3, tiled=True)  69.1 us
    convert_element_type x3, local copies, waits for them, and re-layouts, mode_sum(): term_three.astype(jnp.float32)  67.3 us
    all_to_all x2, blocking collectives, mode_sum(): term_three = lax.all_to_all(part_three, 'mode3', 3, 2, tiled=True)  36.4 us
  transfers between devices with their start and end apart: 8, of which 6 were waited for; matrix products, arithmetic and copies ran while one was open for 32% of the time, Pallas kernels for 0%

commit v1 on v0

v1 whole, which is shorter than its diff:
```python
import functools

import jax
import jax.numpy as jnp
from jax import lax
from jax.experimental import pallas as pl
from jax.experimental.pallas import tpu as pltpu
from jax.sharding import PartitionSpec as P

BF16, F32 = jnp.bfloat16, jnp.float32
AHEAD = 3
SLOTS = 2


def kernel(n1, n2, x, d, a1, a2, a3, b1, b2, b3, z, w, ly, lx, lc, ty, tx,
           f1, f2, g, dv, perm, buf_y, buf_x, mid_a, mid_b, out_y, out_x, vb, cb, yb, xb, ws, zs,
           in_send, in_recv, out_send, out_recv, own_sem, ld):
    rhs, len_i, len_j, len_k = x.shape
    blk_j, blk_i = len_j // n1, len_i // n2
    me_y, me_x, me_c = lax.axis_index('mode1'), lax.axis_index('mode2'), lax.axis_index('mode3')
    other = 1 - me_c
    order_y = [o for o in (1, n1 - 1, *range(2, n1 - 1))]
    order_x = [o for o in (1, n2 - 1, *range(2, n2 - 1))]

    def peer_y(o):
        return lax.rem(me_y + o, n1)

    def peer_x(o):
        return lax.rem(me_x + o, n2)

    def al(v, m):
        return pl.multiple_of(v * m, m)

    def remote(src, dst, send, recv, axis, index):
        return pltpu.make_async_remote_copy(src_ref=src, dst_ref=dst, send_sem=send, recv_sem=recv,
                                            device_id={axis: index}, device_id_type=pl.DeviceIdType.MESH)

    def in_copies(s, v, r):
        y_list, x_list = [], []
        for o in order_y:
            q = peer_y(o)
            y_list.append(remote(v.at[r, :, pl.ds(al(q, blk_j), blk_j), :], ly.at[s, r, pl.ds(al(me_y, len_i), len_i)],
                                 in_send.at[s, r, o - 1], in_recv.at[s, r, o - 1], 'mode1', q))
        for o in order_x:
            p = peer_x(o)
            x_list.append(remote(v.at[r, pl.ds(al(p, blk_i), blk_i)], lx.at[s, r, :, pl.ds(al(me_x, len_j), len_j), :],
                                 in_send.at[s, r, n1 + o - 2], in_recv.at[s, r, n1 + o - 2], 'mode2', p))
        core = remote(v.at[r], lc.at[s, r], in_send.at[s, r, n1 + n2 - 2], in_recv.at[s, r, n1 + n2 - 2], 'mode3', other)
        return y_list, x_list, core

    def send_in(s, v, r):
        y_list, x_list, core = in_copies(s, v, r)
        for pair in zip(x_list, y_list):
            for copy in pair:
                copy.start()
        core.start()

    def out_x_copies(s, r, slot):
        copies = []
        for o in order_x:
            p = peer_x(o)
            copies.append(remote(out_x.at[s, slot, :, pl.ds(al(p, len_j), len_j), :], tx.at[s, r, pl.ds(al(me_x, blk_i), blk_i)],
                                 out_send.at[s, r, n1 + o - 2], out_recv.at[s, r, n1 + o - 2], 'mode2', p))
        own = pltpu.make_async_copy(out_x.at[s, slot, :, pl.ds(al(me_x, len_j), len_j), :],
                                    tx.at[s, r, pl.ds(al(me_x, blk_i), blk_i)], own_sem.at[s, slot, 1])
        return copies, own

    def out_y_copies(s, r, slot):
        copies = []
        for o in order_y:
            q = peer_y(o)
            copies.append(remote(out_y.at[s, slot, pl.ds(al(q, len_i), len_i)], ty.at[s, r, :, pl.ds(al(me_y, blk_j), blk_j), :],
                                 out_send.at[s, r, o - 1], out_recv.at[s, r, o - 1], 'mode1', q))
        own = pltpu.make_async_copy(out_y.at[s, slot, pl.ds(al(me_y, len_i), len_i)],
                                    ty.at[s, r, :, pl.ds(al(me_y, blk_j), blk_j), :], own_sem.at[s, slot, 0])
        return copies, own

    def products(s, v, r):
        slot = lax.rem(r, SLOTS)
        y_list, x_list, _ = in_copies(s, v, r)
        for copy in x_list + y_list:
            copy.wait_send()
            copy.wait_recv()
        loads = []
        for o in range(n2):
            p = peer_x(o)
            src = v.at[r, pl.ds(al(me_x, blk_i), blk_i)] if o == 0 else lx.at[s, r, :, pl.ds(al(p, len_j), len_j), :]
            loads.append(pltpu.make_async_copy(src, buf_x.at[:, pl.ds(al(p, len_j), len_j), :], ld.at[n1 + o]))
        for o in range(n1):
            q = peer_y(o)
            src = v.at[r, :, pl.ds(al(me_y, blk_j), blk_j), :] if o == 0 else ly.at[s, r, pl.ds(al(q, len_i), len_i)]
            loads.append(pltpu.make_async_copy(src, buf_y.at[pl.ds(al(q, len_i), len_i)], ld.at[o]))
        for copy in loads:
            copy.start()
        for copy in loads[:n2]:
            copy.wait()

        @pl.loop(0, blk_i)
        def _(i):
            out_x[s, slot, i] = jnp.dot(f2[s], buf_x[i], preferred_element_type=F32).astype(BF16)

        copies, own = out_x_copies(s, r, slot)
        for copy in copies + [own]:
            copy.start()
        for copy in loads[n2:]:
            copy.wait()

        blocks = buf_y.shape[0] // blk_j

        @pl.loop(0, blocks)
        def _(b):
            rows = pl.ds(al(b, blk_j), blk_j)
            block = buf_y[rows].reshape(blk_j * blk_j, len_k)
            mid_a[:, rows, :] = jnp.dot(perm[...], block, preferred_element_type=F32).astype(BF16).reshape(blk_j, blk_j, len_k)

        @pl.loop(0, blk_j)
        def _(j):
            mid_b[j] = jnp.dot(f1[s], mid_a[j], preferred_element_type=F32).astype(BF16)

        @pl.loop(0, blocks)
        def _(b):
            rows = pl.ds(al(b, blk_j), blk_j)
            block = mid_b[:, rows, :].reshape(blk_j * blk_j, len_k)
            out_y[s, slot, rows] = jnp.dot(perm[...], block, preferred_element_type=F32).astype(BF16).reshape(blk_j, blk_j, len_k)

        copies, own = out_y_copies(s, r, slot)
        for copy in copies + [own]:
            copy.start()

    def combine(s, v, r):
        slot = lax.rem(r, SLOTS)
        core = in_copies(s, v, r)[2]
        core.wait_send()
        core.wait_recv()
        copies_x, own_x = out_x_copies(s, r, slot)
        copies_y, own_y = out_y_copies(s, r, slot)
        for copy in copies_x + copies_y:
            copy.wait_send()
            copy.wait_recv()
        own_x.wait()
        own_y.wait()
        loads = [pltpu.make_async_copy(src, dst, ld.at[n]) for n, (src, dst) in enumerate(
            ((v.at[r], vb), (lc.at[s, r], cb), (ty.at[s, r], yb), (tx.at[s, r], xb)))]
        for copy in loads:
            copy.start()
        for copy in loads:
            copy.wait()
        step = max(1, 256 // len_j)
        flat = (step * len_j, len_k)

        @pl.loop(0, len_i // step)
        def _(b):
            rows = pl.ds(b * step, step)
            third = (jnp.dot(vb[rows].reshape(flat), g[s, 0], preferred_element_type=F32)
                     + jnp.dot(cb[rows].reshape(flat), g[s, 1], preferred_element_type=F32)).astype(BF16)
            total = (yb[rows].reshape(flat).astype(F32) + xb[rows].reshape(flat).astype(F32)) + third.astype(F32)
            if s == 0:
                scaled = dv[rows].reshape(flat) * total.astype(BF16).astype(F32)
                ws[rows] = scaled.astype(BF16).reshape(step, len_j, len_k)
            else:
                zs[rows] = total.reshape(step, len_j, len_k)

        store = pltpu.make_async_copy(ws, w.at[r], ld.at[0]) if s == 0 else pltpu.make_async_copy(zs, z.at[r], ld.at[0])
        store.start()
        store.wait()

    barrier = pltpu.get_barrier_semaphore()
    for o in range(1, n1):
        pl.semaphore_signal(barrier, inc=1, device_id={'mode1': peer_y(o)}, device_id_type=pl.DeviceIdType.MESH)
    for o in range(1, n2):
        pl.semaphore_signal(barrier, inc=1, device_id={'mode2': peer_x(o)}, device_id_type=pl.DeviceIdType.MESH)
    pl.semaphore_signal(barrier, inc=1, device_id={'mode3': other}, device_id_type=pl.DeviceIdType.MESH)
    pl.semaphore_wait(barrier, n1 + n2 - 1)

    for r in range(AHEAD):
        send_in(0, x, r)

    mine, theirs = pl.ds(al(me_c, len_k), len_k), pl.ds(al(other, len_k), len_k)
    loads = [pltpu.make_async_copy(src, dst, ld.at[n]) for n, (src, dst) in enumerate((
        (a1, f1.at[0]), (b1, f1.at[1]), (a2, f2.at[0]), (b2, f2.at[1]), (d, dv),
        (a3.at[mine, mine], g.at[0, 0]), (a3.at[mine, theirs], g.at[0, 1]),
        (b3.at[mine, mine], g.at[1, 0]), (b3.at[mine, theirs], g.at[1, 1])))]
    for copy in loads:
        copy.start()
    size = blk_j * blk_j
    row = lax.broadcasted_iota(jnp.int32, (size, size), 0)
    col = lax.broadcasted_iota(jnp.int32, (size, size), 1)
    perm[...] = jnp.where(col == lax.rem(row, blk_j) * blk_j + row // blk_j, 1.0, 0.0).astype(BF16)
    for copy in loads:
        copy.wait()
    for s in range(2):
        for c in range(2):
            g[s, c] = g[s, c].astype(F32).T.astype(BF16)

    @pl.loop(0, rhs + 3)
    def _(n):
        @pl.when(n < rhs)
        def _():
            products(0, x, n)

        @pl.when(n + AHEAD < rhs)
        def _():
            send_in(0, x, n + AHEAD)

        @pl.when((n >= 1) & (n < rhs + 1))
        def _():
            combine(0, x, n - 1)
            send_in(1, w, n - 1)

        @pl.when((n >= 2) & (n < rhs + 2))
        def _():
            products(1, w, n - 2)

        @pl.when(n >= 3)
        def _():
            combine(1, w, n - 3)


def solution(mesh):
    n1, n2, n3 = mesh.shape['mode1'], mesh.shape['mode2'], mesh.shape['mode3']
    vol_spec = P('rhs', 'mode1', 'mode2', 'mode3')
    diag_spec = P('mode1', 'mode2', 'mode3')

    def local_op(x_vol, diag_vals, a1, a2, a3, b1, b2, b3):
        rhs, len_i, len_j, len_k = x_vol.shape
        m1, m2 = len_i * n1, len_j * n2
        blk_j, blk_i = len_j // n1, len_i // n2
        any_spec = pl.BlockSpec(memory_space=pl.ANY)
        outs = [
            jax.ShapeDtypeStruct((rhs, len_i, len_j, len_k), F32),
            jax.ShapeDtypeStruct((rhs, len_i, len_j, len_k), BF16),
            jax.ShapeDtypeStruct((2, rhs, m1, blk_j, len_k), BF16),
            jax.ShapeDtypeStruct((2, rhs, blk_i, m2, len_k), BF16),
            jax.ShapeDtypeStruct((2, rhs, len_i, len_j, len_k), BF16),
            jax.ShapeDtypeStruct((2, rhs, len_i, len_j, len_k), BF16),
            jax.ShapeDtypeStruct((2, rhs, len_i, len_j, len_k), BF16),
        ]
        vmem, dma = pltpu.VMEM, pltpu.SemaphoreType.DMA
        local = (len_i, len_j, len_k)
        return pl.pallas_call(
            functools.partial(kernel, n1, n2),
            out_shape=outs,
            in_specs=[any_spec] * 8,
            out_specs=[any_spec] * len(outs),
            scratch_shapes=[
                vmem((2, m1, m1), BF16), vmem((2, m2, m2), BF16), vmem((2, 2, len_k, len_k), BF16), vmem(local, F32),
                vmem((blk_j * blk_j, blk_j * blk_j), BF16),
                vmem((m1, blk_j, len_k), BF16), vmem((blk_i, m2, len_k), BF16),
                vmem((blk_j, m1, len_k), BF16), vmem((blk_j, m1, len_k), BF16),
                vmem((2, SLOTS, m1, blk_j, len_k), BF16), vmem((2, SLOTS, blk_i, m2, len_k), BF16),
                vmem(local, BF16), vmem(local, BF16), vmem(local, BF16), vmem(local, BF16),
                vmem(local, BF16), vmem(local, F32),
                dma((2, rhs, n1 + n2 - 1)), dma((2, rhs, n1 + n2 - 1)),
                dma((2, rhs, n1 + n2 - 2)), dma((2, rhs, n1 + n2 - 2)),
                dma((2, SLOTS, 2)), dma((12,)),
            ],
            compiler_params=pltpu.CompilerParams(collective_id=0, has_side_effects=True, vmem_limit_bytes=60 * 1024 * 1024),
            name='kron',
        )(x_vol, diag_vals, a1, a2, a3, b1, b2, b3)[0]

    return jax.shard_map(local_op, mesh=mesh, in_specs=(vol_spec, diag_spec, P(), P(), P(), P(), P(), P()), out_specs=vol_spec, check_vma=False)
```

time: 1270 us -> 390 us (0.31)
  local copies, waits for them, and re-layouts: 603 us -> 11.8 us
  waiting for transfers between devices: 398 us -> 0 us
  Pallas kernels: 0 us -> 377 us
  other arithmetic: 79.8 us -> 0 us
  matrix products: 70.1 us -> 0 us
  blocking collectives: 60.7 us -> 0 us
  starting transfers between devices: 46.6 us -> 0 us
    all_to_all x8 -> x0, waiting for transfers between devices: 398 us -> none  [the longest x2 173 us: mode_sum(): whole_one = lax.all_to_all(volume, 'mode1', 2, 1, tiled=True)]
    pallas_call x0 -> x1, Pallas kernels: none -> 377 us  [local_op(): pl.pallas_call(functools.partial(kernel, n1, n2), out_shape=outs, in_spec...]
    convert_element_type x15 -> x0, local copies, waits for them, and re-layouts: 263 us -> none  [the longest x2 88.6 us: mode_sum(): jnp.einsum('rijc,kc->rijk', whole_three, mat_three, preferred_element_typ...]
    all_to_all x13 -> x0, local copies, waits for them, and re-layouts: 188 us -> none  [the longest x4 69.1 us: mode_sum(): whole_three = lax.all_to_all(volume, 'mode3', 2, 3, tiled=True)]
    unnamed x22 -> x1, local copies, waits for them, and re-layouts: 151 us -> 11.8 us
    dot_general x6 -> x0, matrix products: 70.1 us -> none  [the longest x2 31.5 us: mode_sum(): jnp.einsum('ia,rajk->rijk', mat_one, whole_one, preferred_element_type=jn...]
    convert_element_type x5 -> x0, other arithmetic: 62.7 us -> none  [the longest x2 23.7 us: mode_sum(): term_one.astype(jnp.float32) + term_two.astype(jnp.float32)]
    all_to_all x4 -> x0, blocking collectives: 60.7 us -> none  [the longest x2 36.4 us: mode_sum(): term_three = lax.all_to_all(part_three, 'mode3', 3, 2, tiled=True)]
  transfers between devices with their start and end apart: 8 -> 0, of which waited for: 6 -> 0; matrix products, arithmetic and copies ran while one was open for 32% -> 0% of each run, Pallas kernels for 0% -> 0%
where the time goes in v1:
time: 390 us; the launch traced here: 389 us
  Pallas kernels  377 us (97%)
  local copies, waits for them, and re-layouts  11.8 us (3%)
    pallas_call x1, Pallas kernels, local_op(): pl.pallas_call(functools.partial(kernel, n1, n2), out_shape=outs, in_spec...  377 us
    unnamed x1, local copies, waits for them, and re-layouts  11.8 us

profile of v1, /device:TPU:96, one launch (start us, length us, event | category | flops | bytes accessed | tf_op | source)
XLA Modules:
  0.0 389.0 jit_solution(260381937315578358)
XLA Ops:
  0.0 377.2 %kron.1 = (f32[8,32,64,256]{3,2,1,0:T(8,128)}, bf16[8,32,64,256]{3,2,1,0:T(8,128)(2,1)}, bf16[2,8,128,16,256]{4,3,2,1,0:T(8,128)(2,1)}, bf16[2,8,8,256,256]{4,3,...) custom-call(bf16[8,32,64,256]{3,2,1,0:T(8,128)(2,1)} %x.1, ...), custom_call_target="tpu_custom_call" | custom-call | tf_op jit(solution)/shard_map/kron/pallas_call | solution.py:240
  377.2 11.8 %copy.10 = f32[8,32,64,256]{3,2,1,0:T(8,128)} copy(f32[8,32,64,256]{3,2,1,0:T(8,128)} %get-tuple-element.6) | data formatting | bytes 33554432

commit v2 on v1

--- a/solution.py
+++ b/solution.py
@@ -12,8 +12,8 @@
 SLOTS = 2
 
 
-def kernel(n1, n2, x, d, a1, a2, a3, b1, b2, b3, z, w, ly, lx, lc, ty, tx,
-           f1, f2, g, dv, perm, buf_y, buf_x, mid_a, mid_b, out_y, out_x, vb, cb, yb, xb, ws, zs,
+def kernel(n1, n2, x, d, a1, a2, a3, b1, b2, b3, z, third_last, w, ly, lx, lc, ty, tx,
+           f1, f2, g, dv, perm, buf_y, buf_x, mid_a, mid_b, out_y, out_x, vb, cb, yb, xb, ws,
            in_send, in_recv, out_send, out_recv, own_sem, ld):
     rhs, len_i, len_j, len_k = x.shape
     blk_j, blk_i = len_j // n1, len_i // n2
@@ -127,11 +127,16 @@
         for copy in copies + [own]:
             copy.start()
 
-    def combine(s, v, r):
-        slot = lax.rem(r, SLOTS)
+    step = max(1, 256 // len_j)
+    flat = (step * len_j, len_k)
+
+    def wait_core(s, v, r):
         core = in_copies(s, v, r)[2]
         core.wait_send()
         core.wait_recv()
+
+    def wait_out(s, r):
+        slot = lax.rem(r, SLOTS)
         copies_x, own_x = out_x_copies(s, r, slot)
         copies_y, own_y = out_y_copies(s, r, slot)
         for copy in copies_x + copies_y:
@@ -139,30 +144,35 @@
             copy.wait_recv()
         own_x.wait()
         own_y.wait()
+
+    def mode3(s, rows):
+        return (jnp.dot(vb[rows].reshape(flat), g[s, 0], preferred_element_type=F32)
+                + jnp.dot(cb[rows].reshape(flat), g[s, 1], preferred_element_type=F32)).astype(BF16)
+
+    def combine(s, v, r):
+        wait_core(s, v, r)
+        wait_out(s, r)
         loads = [pltpu.make_async_copy(src, dst, ld.at[n]) for n, (src, dst) in enumerate(
             ((v.at[r], vb), (lc.at[s, r], cb), (ty.at[s, r], yb), (tx.at[s, r], xb)))]
         for copy in loads:
             copy.start()
         for copy in loads:
             copy.wait()
-        step = max(1, 256 // len_j)
-        flat = (step * len_j, len_k)
 
         @pl.loop(0, len_i // step)
         def _(b):
             rows = pl.ds(b * step, step)
-            third = (jnp.dot(vb[rows].reshape(flat), g[s, 0], preferred_element_type=F32)
-                     + jnp.dot(cb[rows].reshape(flat), g[s, 1], preferred_element_type=F32)).astype(BF16)
-            total = (yb[rows].reshape(flat).astype(F32) + xb[rows].reshape(flat).astype(F32)) + third.astype(F32)
+            total = (yb[rows].reshape(flat).astype(F32) + xb[rows].reshape(flat).astype(F32)) + mode3(s, rows).astype(F32)
             if s == 0:
                 scaled = dv[rows].reshape(flat) * total.astype(BF16).astype(F32)
                 ws[rows] = scaled.astype(BF16).reshape(step, len_j, len_k)
             else:
-                zs[rows] = total.reshape(step, len_j, len_k)
-
-        store = pltpu.make_async_copy(ws, w.at[r], ld.at[0]) if s == 0 else pltpu.make_async_copy(zs, z.at[r], ld.at[0])
-        store.start()
-        store.wait()
+                z[r, rows] = total.reshape(step, len_j, len_k)
+
+        if s == 0:
+            store = pltpu.make_async_copy(ws, w.at[r], ld.at[0])
+            store.start()
+            store.wait()
 
     barrier = pltpu.get_barrier_semaphore()
     for o in range(1, n1):
@@ -192,7 +202,7 @@
         for c in range(2):
             g[s, c] = g[s, c].astype(F32).T.astype(BF16)
 
-    @pl.loop(0, rhs + 3)
+    @pl.loop(0, rhs + 2)
     def _(n):
         @pl.when(n < rhs)
         def _():
@@ -211,9 +221,45 @@
         def _():
             products(1, w, n - 2)
 
-        @pl.when(n >= 3)
+        @pl.when((n >= 3) & (n < rhs + 2))
         def _():
             combine(1, w, n - 3)
+
+    last = rhs - 1
+    wait_core(1, w, last)
+    loads = [pltpu.make_async_copy(w.at[last], vb, ld.at[0]), pltpu.make_async_copy(lc.at[1, last], cb, ld.at[1])]
+    for copy in loads:
+        copy.start()
+    for copy in loads:
+        copy.wait()
+
+    @pl.loop(0, len_i // step)
+    def _(b):
+        rows = pl.ds(b * step, step)
+        third_last[rows] = mode3(1, rows).reshape(step, len_j, len_k)
+
+    wait_out(1, last)
+
+
+def finish(z_first, third, ty, tx, z, yb, xb, zb, sem):
+    done, len_i = z_first.shape[0], z_first.shape[1]
+    loads = [pltpu.make_async_copy(ty.at[1, done], yb, sem.at[done]), pltpu.make_async_copy(tx.at[1, done], xb, sem.at[done + 1])]
+    for copy in loads:
+        copy.start()
+    writes = [pltpu.make_async_copy(z_first.at[r], z.at[r], sem.at[r]) for r in range(done)]
+    for copy in writes:
+        copy.start()
+    for copy in loads:
+        copy.wait()
+
+    @pl.loop(0, len_i)
+    def _(i):
+        zb[i] = (yb[i].astype(F32) + xb[i].astype(F32)) + third[i].astype(F32)
+
+    writes.append(pltpu.make_async_copy(zb, z.at[done], sem.at[done]))
+    writes[-1].start()
+    for copy in writes:
+        copy.wait()
 
 
 def solution(mesh):
@@ -226,8 +272,10 @@
         m1, m2 = len_i * n1, len_j * n2
         blk_j, blk_i = len_j // n1, len_i // n2
         any_spec = pl.BlockSpec(memory_space=pl.ANY)
+        vmem_spec = pl.BlockSpec(memory_space=pltpu.VMEM)
         outs = [
-            jax.ShapeDtypeStruct((rhs, len_i, len_j, len_k), F32),
+            pltpu.VMEM((rhs - 1, len_i, len_j, len_k), F32),
+            pltpu.VMEM((len_i, len_j, len_k), BF16),
             jax.ShapeDtypeStruct((rhs, len_i, len_j, len_k), BF16),
             jax.ShapeDtypeStruct((2, rhs, m1, blk_j, len_k), BF16),
             jax.ShapeDtypeStruct((2, rhs, blk_i, m2, len_k), BF16),
@@ -237,11 +285,11 @@
         ]
         vmem, dma = pltpu.VMEM, pltpu.SemaphoreType.DMA
         local = (len_i, len_j, len_k)
-        return pl.pallas_call(
+        res = pl.pallas_call(
             functools.partial(kernel, n1, n2),
             out_shape=outs,
             in_specs=[any_spec] * 8,
-            out_specs=[any_spec] * len(outs),
+            out_specs=[vmem_spec] * 2 + [any_spec] * (len(outs) - 2),
             scratch_shapes=[
                 vmem((2, m1, m1), BF16), vmem((2, m2, m2), BF16), vmem((2, 2, len_k, len_k), BF16), vmem(local, F32),
                 vmem((blk_j * blk_j, blk_j * blk_j), BF16),
@@ -249,13 +297,22 @@
                 vmem((blk_j, m1, len_k), BF16), vmem((blk_j, m1, len_k), BF16),
                 vmem((2, SLOTS, m1, blk_j, len_k), BF16), vmem((2, SLOTS, blk_i, m2, len_k), BF16),
                 vmem(local, BF16), vmem(local, BF16), vmem(local, BF16), vmem(local, BF16),
-                vmem(local, BF16), vmem(local, F32),
+                vmem(local, BF16),
                 dma((2, rhs, n1 + n2 - 1)), dma((2, rhs, n1 + n2 - 1)),
                 dma((2, rhs, n1 + n2 - 2)), dma((2, rhs, n1 + n2 - 2)),
                 dma((2, SLOTS, 2)), dma((12,)),
             ],
-            compiler_params=pltpu.CompilerParams(collective_id=0, has_side_effects=True, vmem_limit_bytes=60 * 1024 * 1024),
+            compiler_params=pltpu.CompilerParams(collective_id=0, has_side_effects=True, vmem_limit_bytes=48 * 1024 * 1024),
             name='kron',
-        )(x_vol, diag_vals, a1, a2, a3, b1, b2, b3)[0]
+        )(x_vol, diag_vals, a1, a2, a3, b1, b2, b3)
+        return pl.pallas_call(
+            finish,
+            out_shape=jax.ShapeDtypeStruct(x_vol.shape, F32),
+            in_specs=[vmem_spec] * 2 + [any_spec] * 2,
+            out_specs=any_spec,
+            scratch_shapes=[vmem(local, BF16), vmem(local, BF16), vmem(local, F32), dma((rhs + 1,))],
+            compiler_params=pltpu.CompilerParams(vmem_limit_bytes=48 * 1024 * 1024),
+            name='finish',
+        )(res[0], res[1], res[-2], res[-1])
 
     return jax.shard_map(local_op, mesh=mesh, in_specs=(vol_spec, diag_spec, P(), P(), P(), P(), P(), P()), out_specs=vol_spec, check_vma=False)

time: 390 us -> 389 us (level)
  local copies, waits for them, and re-layouts: 11.8 us -> 5.21 us
  Pallas kernels: 377 us -> 383 us
    pallas_call x0 -> x1, Pallas kernels: none -> 11.2 us  [local_op(): pl.pallas_call(finish, out_shape=jax.ShapeDtypeStruct(x_vol.shape, F32),...]
    unnamed x1 -> x2, local copies, waits for them, and re-layouts: 11.8 us -> 5.21 us
    pallas_call x1, Pallas kernels: 377 us -> 372 us  [local_op(): pl.pallas_call(functools.partial(kernel, n1, n2), out_shape=outs, in_spec...]
where the time goes in v2:
time: 389 us; the launch traced here: 388 us
  Pallas kernels  383 us (98%)
  local copies, waits for them, and re-layouts  5.21 us (1%)
    pallas_call x1, Pallas kernels, local_op(): pl.pallas_call(functools.partial(kernel, n1, n2), out_shape=outs, in_spec...  372 us
    pallas_call x1, Pallas kernels, local_op(): pl.pallas_call(finish, out_shape=jax.ShapeDtypeStruct(x_vol.shape, F32),...  11.2 us

profile of v2, /device:TPU:96, one launch (start us, length us, event | category | flops | bytes accessed | tf_op | source)
XLA Modules:
  0.0 388.3 jit_solution(13789555713330288685)
XLA Ops:
  0.0 371.8 %kron.1 = (f32[7,32,64,256]{3,2,1,0:T(8,128)S(1)}, bf16[32,64,256]{2,1,0:T(8,128)(2,1)S(1)}, bf16[8,32,64,256]{3,2,1,0:T(8,128)(2,1)}, bf16[2,8,128,16,256]{4,3,...) custom-call(bf16[8,32,64,256]{3,2,1,0:T(8,128)(2,1)} %x.1, ...), custom_call_target="tpu_custom_call" | custom-call | tf_op jit(solution)/shard_map/kron/pallas_call | solution.py:288
  371.9 0.0 copy-start
  371.9 5.2 %copy-done = f32[7,32,64,256]{3,2,1,0:T(8,128)} copy-done((f32[7,32,64,256]{3,2,1,0:T(8,128)}, f32[7,32,64,256]{3,2,1,0:T(8,128)S(1)}, u32[]{:S(2)}) %copy-start) | copy-done | bytes 14680088
  377.1 11.2 %finish.1 = f32[8,32,64,256]{3,2,1,0:T(8,128)} custom-call(f32[7,32,64,256]{3,2,1,0:T(8,128)} %copy-done, bf16[32,64,256]{2,1,0:T(8,128)(2,1)S(1)} %get-tuple-element.10.third, bf16[2,8,32,64,256]{4,3,2,1,0:T(8,128)(2,1)} %get-tuple-element.11.ty, bf16[2,8,32,64,256]{4,3,2,1,0:T(8,128)(2,1)} %get-tuple-element.12.tx), custom_call_target="tpu_custom_call" | custom-call | tf_op jit(solution)/shard_map/finish/pallas_call | solution.py:308
Async XLA Ops:
  371.9 5.2 %copy-start = (f32[7,32,64,256]{3,2,1,0:T(8,128)}, f32[7,32,64,256]{3,2,1,0:T(8,128)S(1)}, u32[]{:S(2)}) copy-start(f32[7,32,64,256]{3,2,1,0:T(8,128)S(1)} %get-tuple-element.9.z_first) | copy-start | bytes 44040196

commit v3 on v2

--- a/solution.py
+++ b/solution.py
@@ -12,7 +12,7 @@
 SLOTS = 2
 
 
-def kernel(n1, n2, x, d, a1, a2, a3, b1, b2, b3, z, third_last, w, ly, lx, lc, ty, tx,
+def kernel(n1, n2, x, d, a1, a2, a3, b1, b2, b3, z, third_last, ty_last, tx_last, w, ly, lx, lc, ty, tx,
            f1, f2, g, dv, perm, buf_y, buf_x, mid_a, mid_b, out_y, out_x, vb, cb, yb, xb, ws,
            in_send, in_recv, out_send, out_recv, own_sem, ld):
     rhs, len_i, len_j, len_k = x.shape
@@ -55,27 +55,33 @@
                 copy.start()
         core.start()
 
-    def out_x_copies(s, r, slot):
+    def out_x_copies(s, r, slot, last=False):
         copies = []
+        home = tx_last if last else tx.at[s, r]
         for o in order_x:
             p = peer_x(o)
-            copies.append(remote(out_x.at[s, slot, :, pl.ds(al(p, len_j), len_j), :], tx.at[s, r, pl.ds(al(me_x, blk_i), blk_i)],
+            copies.append(remote(out_x.at[s, slot, :, pl.ds(al(p, len_j), len_j), :], home.at[pl.ds(al(me_x, blk_i), blk_i)],
                                  out_send.at[s, r, n1 + o - 2], out_recv.at[s, r, n1 + o - 2], 'mode2', p))
+        if last:
+            return copies, None
         own = pltpu.make_async_copy(out_x.at[s, slot, :, pl.ds(al(me_x, len_j), len_j), :],
-                                    tx.at[s, r, pl.ds(al(me_x, blk_i), blk_i)], own_sem.at[s, slot, 1])
+                                    home.at[pl.ds(al(me_x, blk_i), blk_i)], own_sem.at[s, slot, 1])
         return copies, own
 
-    def out_y_copies(s, r, slot):
+    def out_y_copies(s, r, slot, last=False):
         copies = []
+        home = ty_last if last else ty.at[s, r]
         for o in order_y:
             q = peer_y(o)
-            copies.append(remote(out_y.at[s, slot, pl.ds(al(q, len_i), len_i)], ty.at[s, r, :, pl.ds(al(me_y, blk_j), blk_j), :],
+            copies.append(remote(out_y.at[s, slot, pl.ds(al(q, len_i), len_i)], home.at[:, pl.ds(al(me_y, blk_j), blk_j), :],
                                  out_send.at[s, r, o - 1], out_recv.at[s, r, o - 1], 'mode1', q))
+        if last:
+            return copies, None
         own = pltpu.make_async_copy(out_y.at[s, slot, pl.ds(al(me_y, len_i), len_i)],
-                                    ty.at[s, r, :, pl.ds(al(me_y, blk_j), blk_j), :], own_sem.at[s, slot, 0])
+                                    home.at[:, pl.ds(al(me_y, blk_j), blk_j), :], own_sem.at[s, slot, 0])
         return copies, own
 
-    def products(s, v, r):
+    def products(s, v, r, last=False):
         slot = lax.rem(r, SLOTS)
         y_list, x_list, _ = in_copies(s, v, r)
         for copy in x_list + y_list:
@@ -99,8 +105,8 @@
         def _(i):
             out_x[s, slot, i] = jnp.dot(f2[s], buf_x[i], preferred_element_type=F32).astype(BF16)
 
-        copies, own = out_x_copies(s, r, slot)
-        for copy in copies + [own]:
+        copies, own = out_x_copies(s, r, slot, last)
+        for copy in copies if last else copies + [own]:
             copy.start()
         for copy in loads[n2:]:
             copy.wait()
@@ -123,9 +129,12 @@
             block = mid_b[:, rows, :].reshape(blk_j * blk_j, len_k)
             out_y[s, slot, rows] = jnp.dot(perm[...], block, preferred_element_type=F32).astype(BF16).reshape(blk_j, blk_j, len_k)
 
-        copies, own = out_y_copies(s, r, slot)
-        for copy in copies + [own]:
+        copies, own = out_y_copies(s, r, slot, last)
+        for copy in copies if last else copies + [own]:
             copy.start()
+        if last:
+            tx_last[pl.ds(al(me_x, blk_i), blk_i)] = out_x[s, slot, :, pl.ds(al(me_x, len_j), len_j), :]
+            ty_last[:, pl.ds(al(me_y, blk_j), blk_j), :] = out_y[s, slot, pl.ds(al(me_y, len_i), len_i)]
 
     step = max(1, 256 // len_j)
     flat = (step * len_j, len_k)
@@ -135,15 +144,16 @@
         core.wait_send()
         core.wait_recv()
 
-    def wait_out(s, r):
+    def wait_out(s, r, last=False):
         slot = lax.rem(r, SLOTS)
-        copies_x, own_x = out_x_copies(s, r, slot)
-        copies_y, own_y = out_y_copies(s, r, slot)
+        copies_x, own_x = out_x_copies(s, r, slot, last)
+        copies_y, own_y = out_y_copies(s, r, slot, last)
         for copy in copies_x + copies_y:
             copy.wait_send()
             copy.wait_recv()
-        own_x.wait()
-        own_y.wait()
+        if not last:
+            own_x.wait()
+            own_y.wait()
 
     def mode3(s, rows):
         return (jnp.dot(vb[rows].reshape(flat), g[s, 0], preferred_element_type=F32)
@@ -202,7 +212,7 @@
         for c in range(2):
             g[s, c] = g[s, c].astype(F32).T.astype(BF16)
 
-    @pl.loop(0, rhs + 2)
+    @pl.loop(0, rhs + 1)
     def _(n):
         @pl.when(n < rhs)
         def _():
@@ -212,20 +222,22 @@
         def _():
             send_in(0, x, n + AHEAD)
 
-        @pl.when((n >= 1) & (n < rhs + 1))
+        @pl.when(n >= 1)
         def _():
             combine(0, x, n - 1)
             send_in(1, w, n - 1)
 
-        @pl.when((n >= 2) & (n < rhs + 2))
+        @pl.when(n >= 2)
         def _():
             products(1, w, n - 2)
 
-        @pl.when((n >= 3) & (n < rhs + 2))
+        @pl.when(n >= 3)
         def _():
             combine(1, w, n - 3)
 
     last = rhs - 1
+    products(1, w, last, True)
+    combine(1, w, last - 1)
     wait_core(1, w, last)
     loads = [pltpu.make_async_copy(w.at[last], vb, ld.at[0]), pltpu.make_async_copy(lc.at[1, last], cb, ld.at[1])]
     for copy in loads:
@@ -238,23 +250,18 @@
         rows = pl.ds(b * step, step)
         third_last[rows] = mode3(1, rows).reshape(step, len_j, len_k)
 
-    wait_out(1, last)
-
-
-def finish(z_first, third, ty, tx, z, yb, xb, zb, sem):
+    wait_out(1, last, True)
+
+
+def finish(z_first, third, ty, tx, z, zb, sem):
     done, len_i = z_first.shape[0], z_first.shape[1]
-    loads = [pltpu.make_async_copy(ty.at[1, done], yb, sem.at[done]), pltpu.make_async_copy(tx.at[1, done], xb, sem.at[done + 1])]
-    for copy in loads:
-        copy.start()
     writes = [pltpu.make_async_copy(z_first.at[r], z.at[r], sem.at[r]) for r in range(done)]
     for copy in writes:
         copy.start()
-    for copy in loads:
-        copy.wait()
 
     @pl.loop(0, len_i)
     def _(i):
-        zb[i] = (yb[i].astype(F32) + xb[i].astype(F32)) + third[i].astype(F32)
+        zb[i] = (ty[i].astype(F32) + tx[i].astype(F32)) + third[i].astype(F32)
 
     writes.append(pltpu.make_async_copy(zb, z.at[done], sem.at[done]))
     writes[-1].start()
@@ -275,7 +282,7 @@
         vmem_spec = pl.BlockSpec(memory_space=pltpu.VMEM)
         outs = [
             pltpu.VMEM((rhs - 1, len_i, len_j, len_k), F32),
-            pltpu.VMEM((len_i, len_j, len_k), BF16),
+            *[pltpu.VMEM((len_i, len_j, len_k), BF16)] * 3,
             jax.ShapeDtypeStruct((rhs, len_i, len_j, len_k), BF16),
             jax.ShapeDtypeStruct((2, rhs, m1, blk_j, len_k), BF16),
             jax.ShapeDtypeStruct((2, rhs, blk_i, m2, len_k), BF16),
@@ -289,7 +296,7 @@
             functools.partial(kernel, n1, n2),
             out_shape=outs,
             in_specs=[any_spec] * 8,
-            out_specs=[vmem_spec] * 2 + [any_spec] * (len(outs) - 2),
+            out_specs=[vmem_spec] * 4 + [any_spec] * (len(outs) - 4),
             scratch_shapes=[
                 vmem((2, m1, m1), BF16), vmem((2, m2, m2), BF16), vmem((2, 2, len_k, len_k), BF16), vmem(local, F32),
                 vmem((blk_j * blk_j, blk_j * blk_j), BF16),
@@ -302,17 +309,17 @@
                 dma((2, rhs, n1 + n2 - 2)), dma((2, rhs, n1 + n2 - 2)),
                 dma((2, SLOTS, 2)), dma((12,)),
             ],
-            compiler_params=pltpu.CompilerParams(collective_id=0, has_side_effects=True, vmem_limit_bytes=48 * 1024 * 1024),
+            compiler_params=pltpu.CompilerParams(collective_id=0, has_side_effects=True, vmem_limit_bytes=46 * 1024 * 1024),
             name='kron',
         )(x_vol, diag_vals, a1, a2, a3, b1, b2, b3)
         return pl.pallas_call(
             finish,
             out_shape=jax.ShapeDtypeStruct(x_vol.shape, F32),
-            in_specs=[vmem_spec] * 2 + [any_spec] * 2,
+            in_specs=[vmem_spec] * 4,
             out_specs=any_spec,
-            scratch_shapes=[vmem(local, BF16), vmem(local, BF16), vmem(local, F32), dma((rhs + 1,))],
-            compiler_params=pltpu.CompilerParams(vmem_limit_bytes=48 * 1024 * 1024),
+            scratch_shapes=[vmem(local, F32), dma((rhs,))],
+            compiler_params=pltpu.CompilerParams(vmem_limit_bytes=8 * 1024 * 1024),
             name='finish',
-        )(res[0], res[1], res[-2], res[-1])
+        )(*res[:4])
 
     return jax.shard_map(local_op, mesh=mesh, in_specs=(vol_spec, diag_spec, P(), P(), P(), P(), P(), P()), out_specs=vol_spec, check_vma=False)

time: 389 us -> 379 us (0.974)
  local copies, waits for them, and re-layouts: 5.21 us -> 0 us
  Pallas kernels: 383 us -> 378 us
    pallas_call x1, Pallas kernels: 11.2 us -> 5.93 us  [local_op(): pl.pallas_call(finish, out_shape=jax.ShapeDtypeStruct(x_vol.shape, F32),...]
    unnamed x2 -> x0, local copies, waits for them, and re-layouts: 5.21 us -> none
where the time goes in v3:
time: 379 us; the launch traced here: 378 us
  Pallas kernels  378 us (100%)
    pallas_call x1, Pallas kernels, local_op(): pl.pallas_call(functools.partial(kernel, n1, n2), out_shape=outs, in_spec...  372 us

profile of v3, /device:TPU:96, one launch (start us, length us, event | category | flops | bytes accessed | tf_op | source)
XLA Modules:
  0.0 377.8 jit_solution(15686935249558369974)
XLA Ops:
  0.0 371.8 %kron.1 = (f32[7,32,64,256]{3,2,1,0:T(8,128)S(1)}, bf16[32,64,256]{2,1,0:T(8,128)(2,1)S(1)}, bf16[32,64,256]{2,1,0:T(8,128)(2,1)S(1)}, bf16[32,64,256]{2,1,0:T(8...) custom-call(bf16[8,32,64,256]{3,2,1,0:T(8,128)(2,1)} %x.1, ...), custom_call_target="tpu_custom_call" | custom-call | tf_op jit(solution)/shard_map/kron/pallas_call | solution.py:295
  371.8 5.9 %finish.1 = f32[8,32,64,256]{3,2,1,0:T(8,128)} custom-call(f32[7,32,64,256]{3,2,1,0:T(8,128)S(1)} %get-tuple-element.9.z_first, bf16[32,64,256]{2,1,0:T(8,128)(2,1)S(1)} %get-tuple-element.10.third, bf16[32,64,256]{2,1,0:T(8,128)(2,1)S(1)} %get-tuple-element.11.ty, bf16[32,64,256]{2,1,0:T(8,128)(2,1)S(1)} %get-tuple-element.12.tx), custom_call_target="tpu_custom_call" | custom-call | tf_op jit(solution)/shard_map/finish/pallas_call | solution.py:315

commit v4 on v3

v4 whole, which is shorter than its diff:
```python
import functools

import jax
import jax.numpy as jnp
from jax import lax
from jax.experimental import pallas as pl
from jax.experimental.pallas import tpu as pltpu
from jax.sharding import PartitionSpec as P

BF16, F32 = jnp.bfloat16, jnp.float32
AHEAD = 2
SLOTS = 2
PER = 2


def kernel(n1, n2, x, d, a1, a2, a3, b1, b2, b3, z, third_last, ty_last, tx_last, w, ly, lx, lc, ty, tx,
           f1, f2, g, dv, perm, buf_y, buf_x, mid_a, mid_b, out_y, out_x, vb, cb, yb, xb, ws,
           in_send, in_recv, out_send, out_recv, own_sem, ld):
    rhs, len_i, len_j, len_k = x.shape
    blk_j, blk_i = len_j // n1, len_i // n2
    me_y, me_x, me_c = lax.axis_index('mode1'), lax.axis_index('mode2'), lax.axis_index('mode3')
    other = 1 - me_c
    chunks = rhs // PER
    order_y = [o for o in (1, n1 - 1, *range(2, n1 - 1))]
    order_x = [o for o in (1, n2 - 1, *range(2, n2 - 1))]

    def peer_y(o):
        return lax.rem(me_y + o, n1)

    def peer_x(o):
        return lax.rem(me_x + o, n2)

    def al(v, m):
        return pl.multiple_of(v * m, m)

    def remote(src, dst, send, recv, axis, index):
        return pltpu.make_async_remote_copy(src_ref=src, dst_ref=dst, send_sem=send, recv_sem=recv,
                                            device_id={axis: index}, device_id_type=pl.DeviceIdType.MESH)

    def in_copies(s, v, r):
        y_list, x_list = [], []
        group = pl.ds(r * PER, PER)
        for o in order_y:
            q = peer_y(o)
            y_list.append(remote(v.at[group, :, pl.ds(al(q, blk_j), blk_j), :], ly.at[s, group, pl.ds(al(me_y, len_i), len_i)],
                                 in_send.at[s, r, o - 1], in_recv.at[s, r, o - 1], 'mode1', q))
        for o in order_x:
            p = peer_x(o)
            x_list.append(remote(v.at[group, pl.ds(al(p, blk_i), blk_i)], lx.at[s, group, :, pl.ds(al(me_x, len_j), len_j), :],
                                 in_send.at[s, r, n1 + o - 2], in_recv.at[s, r, n1 + o - 2], 'mode2', p))
        core = remote(v.at[group], lc.at[s, group], in_send.at[s, r, n1 + n2 - 2], in_recv.at[s, r, n1 + n2 - 2], 'mode3', other)
        return y_list, x_list, core

    def send_in(s, v, r):
        y_list, x_list, core = in_copies(s, v, r)
        for pair in zip(x_list, y_list):
            for copy in pair:
                copy.start()
        core.start()

    def out_x_copies(s, r, slot, last=False):
        copies = []
        home = tx_last if last else tx.at[s, pl.ds(r * PER, PER)]
        for o in order_x:
            p = peer_x(o)
            copies.append(remote(out_x.at[s, slot, :, :, pl.ds(al(p, len_j), len_j), :], home.at[:, pl.ds(al(me_x, blk_i), blk_i)],
                                 out_send.at[s, r, n1 + o - 2], out_recv.at[s, r, n1 + o - 2], 'mode2', p))
        if last:
            return copies, None
        own = pltpu.make_async_copy(out_x.at[s, slot, :, :, pl.ds(al(me_x, len_j), len_j), :],
                                    home.at[:, pl.ds(al(me_x, blk_i), blk_i)], own_sem.at[s, slot, 1])
        return copies, own

    def out_y_copies(s, r, slot, last=False):
        copies = []
        home = ty_last if last else ty.at[s, pl.ds(r * PER, PER)]
        for o in order_y:
            q = peer_y(o)
            copies.append(remote(out_y.at[s, slot, :, pl.ds(al(q, len_i), len_i)], home.at[:, :, pl.ds(al(me_y, blk_j), blk_j), :],
                                 out_send.at[s, r, o - 1], out_recv.at[s, r, o - 1], 'mode1', q))
        if last:
            return copies, None
        own = pltpu.make_async_copy(out_y.at[s, slot, :, pl.ds(al(me_y, len_i), len_i)],
                                    home.at[:, :, pl.ds(al(me_y, blk_j), blk_j), :], own_sem.at[s, slot, 0])
        return copies, own

    def products(s, v, r, last=False):
        slot = lax.rem(r, SLOTS)
        y_list, x_list, _ = in_copies(s, v, r)
        for copy in x_list + y_list:
            copy.wait_send()
            copy.wait_recv()
        blocks = buf_y.shape[0] // blk_j

        def loads_of(t):
            first, second = [], []
            for o in range(n2):
                p = peer_x(o)
                src = v.at[t, pl.ds(al(me_x, blk_i), blk_i)] if o == 0 else lx.at[s, t, :, pl.ds(al(p, len_j), len_j), :]
                first.append(pltpu.make_async_copy(src, buf_x.at[:, pl.ds(al(p, len_j), len_j), :], ld.at[n1 + o]))
            for o in range(n1):
                q = peer_y(o)
                src = v.at[t, :, pl.ds(al(me_y, blk_j), blk_j), :] if o == 0 else ly.at[s, t, pl.ds(al(q, len_i), len_i)]
                second.append(pltpu.make_async_copy(src, buf_y.at[pl.ds(al(q, len_i), len_i)], ld.at[o]))
            return first, second

        @pl.loop(0, PER)
        def _(c):
            first, second = loads_of(r * PER + c)
            for copy in first + second:
                copy.start()
            for copy in first:
                copy.wait()

            @pl.loop(0, blk_i)
            def _(i):
                out_x[s, slot, c, i] = jnp.dot(f2[s], buf_x[i], preferred_element_type=F32).astype(BF16)

            for copy in second:
                copy.wait()

            @pl.loop(0, blocks)
            def _(b):
                rows = pl.ds(al(b, blk_j), blk_j)
                block = buf_y[rows].reshape(blk_j * blk_j, len_k)
                mid_a[:, rows, :] = jnp.dot(perm[...], block, preferred_element_type=F32).astype(BF16).reshape(blk_j, blk_j, len_k)

            @pl.loop(0, blk_j)
            def _(j):
                mid_b[j] = jnp.dot(f1[s], mid_a[j], preferred_element_type=F32).astype(BF16)

            @pl.loop(0, blocks)
            def _(b):
                rows = pl.ds(al(b, blk_j), blk_j)
                block = mid_b[:, rows, :].reshape(blk_j * blk_j, len_k)
                out_y[s, slot, c, rows] = jnp.dot(perm[...], block, preferred_element_type=F32).astype(BF16).reshape(blk_j, blk_j, len_k)

        copies_x, own_x = out_x_copies(s, r, slot, last)
        copies_y, own_y = out_y_copies(s, r, slot, last)
        for pair in zip(copies_x, copies_y):
            for copy in pair:
                copy.start()
        if last:
            tx_last[:, pl.ds(al(me_x, blk_i), blk_i)] = out_x[s, slot, :, :, pl.ds(al(me_x, len_j), len_j), :]
            ty_last[:, :, pl.ds(al(me_y, blk_j), blk_j), :] = out_y[s, slot, :, pl.ds(al(me_y, len_i), len_i)]
        else:
            own_x.start()
            own_y.start()

    step = max(1, 256 // len_j)
    flat = (step * len_j, len_k)

    def wait_core(s, v, r):
        core = in_copies(s, v, r)[2]
        core.wait_send()
        core.wait_recv()

    def wait_out(s, r, last=False):
        slot = lax.rem(r, SLOTS)
        copies_x, own_x = out_x_copies(s, r, slot, last)
        copies_y, own_y = out_y_copies(s, r, slot, last)
        for copy in copies_x + copies_y:
            copy.wait_send()
            copy.wait_recv()
        if not last:
            own_x.wait()
            own_y.wait()

    def mode3(s, rows):
        return (jnp.dot(vb[rows].reshape(flat), g[s, 0], preferred_element_type=F32)
                + jnp.dot(cb[rows].reshape(flat), g[s, 1], preferred_element_type=F32)).astype(BF16)

    def combine(s, v, r):
        wait_core(s, v, r)
        wait_out(s, r)

        @pl.loop(0, PER)
        def _(c):
            t = r * PER + c
            loads = [pltpu.make_async_copy(src, dst, ld.at[n]) for n, (src, dst) in enumerate(
                ((v.at[t], vb), (lc.at[s, t], cb), (ty.at[s, t], yb), (tx.at[s, t], xb)))]
            for copy in loads:
                copy.start()
            for copy in loads:
                copy.wait()

            @pl.loop(0, len_i // step)
            def _(b):
                rows = pl.ds(b * step, step)
                total = (yb[rows].reshape(flat).astype(F32) + xb[rows].reshape(flat).astype(F32)) + mode3(s, rows).astype(F32)
                if s == 0:
                    scaled = dv[rows].reshape(flat) * total.astype(BF16).astype(F32)
                    ws[rows] = scaled.astype(BF16).reshape(step, len_j, len_k)
                else:
                    z[t, rows] = total.reshape(step, len_j, len_k)

            if s == 0:
                store = pltpu.make_async_copy(ws, w.at[t], ld.at[0])
                store.start()
                store.wait()

    barrier = pltpu.get_barrier_semaphore()
    for o in range(1, n1):
        pl.semaphore_signal(barrier, inc=1, device_id={'mode1': peer_y(o)}, device_id_type=pl.DeviceIdType.MESH)
    for o in range(1, n2):
        pl.semaphore_signal(barrier, inc=1, device_id={'mode2': peer_x(o)}, device_id_type=pl.DeviceIdType.MESH)
    pl.semaphore_signal(barrier, inc=1, device_id={'mode3': other}, device_id_type=pl.DeviceIdType.MESH)
    pl.semaphore_wait(barrier, n1 + n2 - 1)

    for r in range(AHEAD):
        send_in(0, x, r)

    mine, theirs = pl.ds(al(me_c, len_k), len_k), pl.ds(al(other, len_k), len_k)
    loads = [pltpu.make_async_copy(src, dst, ld.at[n]) for n, (src, dst) in enumerate((
        (a1, f1.at[0]), (b1, f1.at[1]), (a2, f2.at[0]), (b2, f2.at[1]), (d, dv),
        (a3.at[mine, mine], g.at[0, 0]), (a3.at[mine, theirs], g.at[0, 1]),
        (b3.at[mine, mine], g.at[1, 0]), (b3.at[mine, theirs], g.at[1, 1])))]
    for copy in loads:
        copy.start()
    size = blk_j * blk_j
    row = lax.broadcasted_iota(jnp.int32, (size, size), 0)
    col = lax.broadcasted_iota(jnp.int32, (size, size), 1)
    perm[...] = jnp.where(col == lax.rem(row, blk_j) * blk_j + row // blk_j, 1.0, 0.0).astype(BF16)
    for copy in loads:
        copy.wait()
    for s in range(2):
        for c in range(2):
            g[s, c] = g[s, c].astype(F32).T.astype(BF16)

    @pl.loop(0, chunks + 1)
    def _(n):
        @pl.when(n < chunks)
        def _():
            products(0, x, n)

        @pl.when(n + AHEAD < chunks)
        def _():
            send_in(0, x, n + AHEAD)

        @pl.when(n >= 1)
        def _():
            combine(0, x, n - 1)
            send_in(1, w, n - 1)

        @pl.when(n >= 2)
        def _():
            products(1, w, n - 2)

        @pl.when(n >= 3)
        def _():
            combine(1, w, n - 3)

    last = chunks - 1
    products(1, w, last, True)
    combine(1, w, last - 1)
    wait_core(1, w, last)

    @pl.loop(0, PER)
    def _(c):
        t = last * PER + c
        loads = [pltpu.make_async_copy(w.at[t], vb, ld.at[0]), pltpu.make_async_copy(lc.at[1, t], cb, ld.at[1])]
        for copy in loads:
            copy.start()
        for copy in loads:
            copy.wait()

        @pl.loop(0, len_i // step)
        def _(b):
            rows = pl.ds(b * step, step)
            third_last[c, rows] = mode3(1, rows).reshape(step, len_j, len_k)

    wait_out(1, last, True)


def finish(z_first, third, ty, tx, z, zb, sem):
    done, len_i = z_first.shape[0], z_first.shape[1]
    writes = [pltpu.make_async_copy(z_first.at[r], z.at[r], sem.at[r]) for r in range(done)]
    for copy in writes:
        copy.start()
    for c in range(third.shape[0]):
        @pl.loop(0, len_i)
        def _(i):
            zb[c, i] = (ty[c, i].astype(F32) + tx[c, i].astype(F32)) + third[c, i].astype(F32)

        writes.append(pltpu.make_async_copy(zb.at[c], z.at[done + c], sem.at[done + c]))
        writes[-1].start()
    for copy in writes:
        copy.wait()


def solution(mesh):
    n1, n2, n3 = mesh.shape['mode1'], mesh.shape['mode2'], mesh.shape['mode3']
    vol_spec = P('rhs', 'mode1', 'mode2', 'mode3')
    diag_spec = P('mode1', 'mode2', 'mode3')

    def local_op(x_vol, diag_vals, a1, a2, a3, b1, b2, b3):
        rhs, len_i, len_j, len_k = x_vol.shape
        m1, m2 = len_i * n1, len_j * n2
        blk_j, blk_i = len_j // n1, len_i // n2
        any_spec = pl.BlockSpec(memory_space=pl.ANY)
        vmem_spec = pl.BlockSpec(memory_space=pltpu.VMEM)
        outs = [
            pltpu.VMEM((rhs - PER, len_i, len_j, len_k), F32),
            *[pltpu.VMEM((PER, len_i, len_j, len_k), BF16)] * 3,
            jax.ShapeDtypeStruct((rhs, len_i, len_j, len_k), BF16),
            jax.ShapeDtypeStruct((2, rhs, m1, blk_j, len_k), BF16),
            jax.ShapeDtypeStruct((2, rhs, blk_i, m2, len_k), BF16),
            jax.ShapeDtypeStruct((2, rhs, len_i, len_j, len_k), BF16),
            jax.ShapeDtypeStruct((2, rhs, len_i, len_j, len_k), BF16),
            jax.ShapeDtypeStruct((2, rhs, len_i, len_j, len_k), BF16),
        ]
        vmem, dma = pltpu.VMEM, pltpu.SemaphoreType.DMA
        local = (len_i, len_j, len_k)
        res = pl.pallas_call(
            functools.partial(kernel, n1, n2),
            out_shape=outs,
            in_specs=[any_spec] * 8,
            out_specs=[vmem_spec] * 4 + [any_spec] * (len(outs) - 4),
            scratch_shapes=[
                vmem((2, m1, m1), BF16), vmem((2, m2, m2), BF16), vmem((2, 2, len_k, len_k), BF16), vmem(local, F32),
                vmem((blk_j * blk_j, blk_j * blk_j), BF16),
                vmem((m1, blk_j, len_k), BF16), vmem((blk_i, m2, len_k), BF16),
                vmem((blk_j, m1, len_k), BF16), vmem((blk_j, m1, len_k), BF16),
                vmem((2, SLOTS, PER, m1, blk_j, len_k), BF16), vmem((2, SLOTS, PER, blk_i, m2, len_k), BF16),
                vmem(local, BF16), vmem(local, BF16), vmem(local, BF16), vmem(local, BF16),
                vmem(local, BF16),
                dma((2, rhs // PER, n1 + n2 - 1)), dma((2, rhs // PER, n1 + n2 - 1)),
                dma((2, rhs // PER, n1 + n2 - 2)), dma((2, rhs // PER, n1 + n2 - 2)),
                dma((2, SLOTS, 2)), dma((12,)),
            ],
            compiler_params=pltpu.CompilerParams(collective_id=0, has_side_effects=True, vmem_limit_bytes=45 * 1024 * 1024),
            name='kron',
        )(x_vol, diag_vals, a1, a2, a3, b1, b2, b3)
        return pl.pallas_call(
            finish,
            out_shape=jax.ShapeDtypeStruct(x_vol.shape, F32),
            in_specs=[vmem_spec] * 4,
            out_specs=any_spec,
            scratch_shapes=[vmem((PER, *local), F32), dma((rhs,))],
            compiler_params=pltpu.CompilerParams(vmem_limit_bytes=8 * 1024 * 1024),
            name='finish',
        )(*res[:4])

    return jax.shard_map(local_op, mesh=mesh, in_specs=(vol_spec, diag_spec, P(), P(), P(), P(), P(), P()), out_specs=vol_spec, check_vma=False)
```

time: 379 us -> 377 us (level)
  no operation moved by 1% of the time
where the time goes in v4:
time: 377 us; the launch traced here: 376 us
  Pallas kernels  376 us (100%)
    pallas_call x1, Pallas kernels, local_op(): pl.pallas_call(functools.partial(kernel, n1, n2), out_shape=outs, in_spec...  370 us

profile of v4, /device:TPU:96, one launch (start us, length us, event | category | flops | bytes accessed | tf_op | source)
XLA Modules:
  0.0 376.0 jit_solution(13838025417324495022)
XLA Ops:
  0.0 370.1 %kron.1 = (f32[6,32,64,256]{3,2,1,0:T(8,128)S(1)}, bf16[2,32,64,256]{3,2,1,0:T(8,128)(2,1)S(1)}, bf16[2,32,64,256]{3,2,1,0:T(8,128)(2,1)S(1)}, bf16[2,32,64,256]...) custom-call(bf16[8,32,64,256]{3,2,1,0:T(8,128)(2,1)} %x.1, ...), custom_call_target="tpu_custom_call" | custom-call | tf_op jit(solution)/shard_map/kron/pallas_call | solution.py:314
  370.1 5.9 %finish.1 = f32[8,32,64,256]{3,2,1,0:T(8,128)} custom-call(f32[6,32,64,256]{3,2,1,0:T(8,128)S(1)} %get-tuple-element.9.z_first, bf16[2,32,64,256]{3,2,1,0:T(8,128)(2,1)S(1)} %get-tuple-element.10.third, bf16[2,32,64,256]{3,2,1,0:T(8,128)(2,1)S(1)} %get-tuple-element.11.ty, bf16[2,32,64,256]{3,2,1,0:T(8,128)(2,1)S(1)} %get-tuple-element.12.tx), custom_call_target="tpu_custom_call" | custom-call | tf_op jit(solution)/shard_map/finish/pallas_call | solution.py:334

commit v5 on v4

--- a/solution.py
+++ b/solution.py
@@ -21,8 +21,13 @@
     me_y, me_x, me_c = lax.axis_index('mode1'), lax.axis_index('mode2'), lax.axis_index('mode3')
     other = 1 - me_c
     chunks = rhs // PER
-    order_y = [o for o in (1, n1 - 1, *range(2, n1 - 1))]
-    order_x = [o for o in (1, n2 - 1, *range(2, n2 - 1))]
+
+    def send_order(n):
+        near_first, far_first = (1, n - 1, *range(2, n - 1)), (*range(2, n - 1), 1, n - 1)
+        return [a + me_c * (b - a) for a, b in zip(near_first, far_first)]
+
+    order_y, order_x = send_order(n1), send_order(n2)
+    all_y, all_x = range(1, n1), range(1, n2)
 
     def peer_y(o):
         return lax.rem(me_y + o, n1)
@@ -37,14 +42,14 @@
         return pltpu.make_async_remote_copy(src_ref=src, dst_ref=dst, send_sem=send, recv_sem=recv,
                                             device_id={axis: index}, device_id_type=pl.DeviceIdType.MESH)
 
-    def in_copies(s, v, r):
+    def in_copies(s, v, r, offsets_y=all_y, offsets_x=all_x):
         y_list, x_list = [], []
         group = pl.ds(r * PER, PER)
-        for o in order_y:
+        for o in offsets_y:
             q = peer_y(o)
             y_list.append(remote(v.at[group, :, pl.ds(al(q, blk_j), blk_j), :], ly.at[s, group, pl.ds(al(me_y, len_i), len_i)],
                                  in_send.at[s, r, o - 1], in_recv.at[s, r, o - 1], 'mode1', q))
-        for o in order_x:
+        for o in offsets_x:
             p = peer_x(o)
             x_list.append(remote(v.at[group, pl.ds(al(p, blk_i), blk_i)], lx.at[s, group, :, pl.ds(al(me_x, len_j), len_j), :],
                                  in_send.at[s, r, n1 + o - 2], in_recv.at[s, r, n1 + o - 2], 'mode2', p))
@@ -52,16 +57,16 @@
         return y_list, x_list, core
 
     def send_in(s, v, r):
-        y_list, x_list, core = in_copies(s, v, r)
+        y_list, x_list, core = in_copies(s, v, r, order_y, order_x)
         for pair in zip(x_list, y_list):
             for copy in pair:
                 copy.start()
         core.start()
 
-    def out_x_copies(s, r, slot, last=False):
+    def out_x_copies(s, r, slot, last=False, offsets=all_x):
         copies = []
         home = tx_last if last else tx.at[s, pl.ds(r * PER, PER)]
-        for o in order_x:
+        for o in offsets:
             p = peer_x(o)
             copies.append(remote(out_x.at[s, slot, :, :, pl.ds(al(p, len_j), len_j), :], home.at[:, pl.ds(al(me_x, blk_i), blk_i)],
                                  out_send.at[s, r, n1 + o - 2], out_recv.at[s, r, n1 + o - 2], 'mode2', p))
@@ -71,10 +76,10 @@
                                     home.at[:, pl.ds(al(me_x, blk_i), blk_i)], own_sem.at[s, slot, 1])
         return copies, own
 
-    def out_y_copies(s, r, slot, last=False):
+    def out_y_copies(s, r, slot, last=False, offsets=all_y):
         copies = []
         home = ty_last if last else ty.at[s, pl.ds(r * PER, PER)]
-        for o in order_y:
+        for o in offsets:
             q = peer_y(o)
             copies.append(remote(out_y.at[s, slot, :, pl.ds(al(q, len_i), len_i)], home.at[:, :, pl.ds(al(me_y, blk_j), blk_j), :],
                                  out_send.at[s, r, o - 1], out_recv.at[s, r, o - 1], 'mode1', q))
@@ -135,8 +140,8 @@
                 block = mid_b[:, rows, :].reshape(blk_j * blk_j, len_k)
                 out_y[s, slot, c, rows] = jnp.dot(perm[...], block, preferred_element_type=F32).astype(BF16).reshape(blk_j, blk_j, len_k)
 
-        copies_x, own_x = out_x_copies(s, r, slot, last)
-        copies_y, own_y = out_y_copies(s, r, slot, last)
+        copies_x, own_x = out_x_copies(s, r, slot, last, order_x)
+        copies_y, own_y = out_y_copies(s, r, slot, last, order_y)
         for pair in zip(copies_x, copies_y):
             for copy in pair:
                 copy.start()

time: 377 us -> 376 us (level)
  no operation moved by 1% of the time
where the time goes in v5:
time: 376 us; the launch traced here: 375 us
  Pallas kernels  375 us (100%)
    pallas_call x1, Pallas kernels, local_op(): pl.pallas_call(functools.partial(kernel, n1, n2), out_shape=outs, in_spec...  369 us

profile of v5, /device:TPU:96, one launch (start us, length us, event | category | flops | bytes accessed | tf_op | source)
XLA Modules:
  0.0 375.4 jit_solution(11188937728501705182)
XLA Ops:
  0.0 369.5 %kron.1 = (f32[6,32,64,256]{3,2,1,0:T(8,128)S(1)}, bf16[2,32,64,256]{3,2,1,0:T(8,128)(2,1)S(1)}, bf16[2,32,64,256]{3,2,1,0:T(8,128)(2,1)S(1)}, bf16[2,32,64,256]...) custom-call(bf16[8,32,64,256]{3,2,1,0:T(8,128)(2,1)} %x.1, ...), custom_call_target="tpu_custom_call" | custom-call | tf_op jit(solution)/shard_map/kron/pallas_call | solution.py:319
  369.5 5.9 %finish.1 = f32[8,32,64,256]{3,2,1,0:T(8,128)} custom-call(f32[6,32,64,256]{3,2,1,0:T(8,128)S(1)} %get-tuple-element.9.z_first, bf16[2,32,64,256]{3,2,1,0:T(8,128)(2,1)S(1)} %get-tuple-element.10.third, bf16[2,32,64,256]{3,2,1,0:T(8,128)(2,1)S(1)} %get-tuple-element.11.ty, bf16[2,32,64,256]{3,2,1,0:T(8,128)(2,1)S(1)} %get-tuple-element.12.tx), custom_call_target="tpu_custom_call" | custom-call | tf_op jit(solution)/shard_map/finish/pallas_call | solution.py:339

commit v6 on v5

--- a/solution.py
+++ b/solution.py
@@ -10,17 +10,18 @@
 BF16, F32 = jnp.bfloat16, jnp.float32
 AHEAD = 2
 SLOTS = 2
-PER = 2
+PER = 4
 
 
 def kernel(n1, n2, x, d, a1, a2, a3, b1, b2, b3, z, third_last, ty_last, tx_last, w, ly, lx, lc, ty, tx,
-           f1, f2, g, dv, perm, buf_y, buf_x, mid_a, mid_b, out_y, out_x, vb, cb, yb, xb, ws,
+           f1, f2, g, dv, buf_y, buf_x, mid_a, mid_b, out_y, out_x, vb, cb, yb, xb, ws,
            in_send, in_recv, out_send, out_recv, own_sem, ld):
     rhs, len_i, len_j, len_k = x.shape
     blk_j, blk_i = len_j // n1, len_i // n2
     me_y, me_x, me_c = lax.axis_index('mode1'), lax.axis_index('mode2'), lax.axis_index('mode3')
     other = 1 - me_c
     chunks = rhs // PER
+    banks = out_y.shape[0]
 
     def send_order(n):
         near_first, far_first = (1, n - 1, *range(2, n - 1)), (*range(2, n - 1), 1, n - 1)
@@ -68,11 +69,11 @@
         home = tx_last if last else tx.at[s, pl.ds(r * PER, PER)]
         for o in offsets:
             p = peer_x(o)
-            copies.append(remote(out_x.at[s, slot, :, :, pl.ds(al(p, len_j), len_j), :], home.at[:, pl.ds(al(me_x, blk_i), blk_i)],
+            copies.append(remote(out_x.at[s % banks, slot, :, :, pl.ds(al(p, len_j), len_j), :], home.at[:, pl.ds(al(me_x, blk_i), blk_i)],
                                  out_send.at[s, r, n1 + o - 2], out_recv.at[s, r, n1 + o - 2], 'mode2', p))
         if last:
             return copies, None
-        own = pltpu.make_async_copy(out_x.at[s, slot, :, :, pl.ds(al(me_x, len_j), len_j), :],
+        own = pltpu.make_async_copy(out_x.at[s % banks, slot, :, :, pl.ds(al(me_x, len_j), len_j), :],
                                     home.at[:, pl.ds(al(me_x, blk_i), blk_i)], own_sem.at[s, slot, 1])
         return copies, own
 
@@ -81,11 +82,11 @@
         home = ty_last if last else ty.at[s, pl.ds(r * PER, PER)]
         for o in offsets:
             q = peer_y(o)
-            copies.append(remote(out_y.at[s, slot, :, pl.ds(al(q, len_i), len_i)], home.at[:, :, pl.ds(al(me_y, blk_j), blk_j), :],
+            copies.append(remote(out_y.at[s % banks, slot, :, pl.ds(al(q, len_i), len_i)], home.at[:, :, pl.ds(al(me_y, blk_j), blk_j), :],
                                  out_send.at[s, r, o - 1], out_recv.at[s, r, o - 1], 'mode1', q))
         if last:
             return copies, None
-        own = pltpu.make_async_copy(out_y.at[s, slot, :, pl.ds(al(me_y, len_i), len_i)],
+        own = pltpu.make_async_copy(out_y.at[s % banks, slot, :, pl.ds(al(me_y, len_i), len_i)],
                                     home.at[:, :, pl.ds(al(me_y, blk_j), blk_j), :], own_sem.at[s, slot, 0])
         return copies, own
 
@@ -119,7 +120,7 @@
 
             @pl.loop(0, blk_i)
             def _(i):
-                out_x[s, slot, c, i] = jnp.dot(f2[s], buf_x[i], preferred_element_type=F32).astype(BF16)
+                out_x[s % banks, slot, c, i] = jnp.dot(f2[s], buf_x[i], preferred_element_type=F32).astype(BF16)
 
             for copy in second:
                 copy.wait()
@@ -127,8 +128,7 @@
             @pl.loop(0, blocks)
             def _(b):
                 rows = pl.ds(al(b, blk_j), blk_j)
-                block = buf_y[rows].reshape(blk_j * blk_j, len_k)
-                mid_a[:, rows, :] = jnp.dot(perm[...], block, preferred_element_type=F32).astype(BF16).reshape(blk_j, blk_j, len_k)
+                mid_a[:, rows, :] = jnp.swapaxes(buf_y[rows], 0, 1)
 
             @pl.loop(0, blk_j)
             def _(j):
@@ -137,8 +137,7 @@
             @pl.loop(0, blocks)
             def _(b):
                 rows = pl.ds(al(b, blk_j), blk_j)
-                block = mid_b[:, rows, :].reshape(blk_j * blk_j, len_k)
-                out_y[s, slot, c, rows] = jnp.dot(perm[...], block, preferred_element_type=F32).astype(BF16).reshape(blk_j, blk_j, len_k)
+                out_y[s % banks, slot, c, rows] = jnp.swapaxes(mid_b[:, rows, :], 0, 1)
 
         copies_x, own_x = out_x_copies(s, r, slot, last, order_x)
         copies_y, own_y = out_y_copies(s, r, slot, last, order_y)
@@ -146,8 +145,8 @@
             for copy in pair:
                 copy.start()
         if last:
-            tx_last[:, pl.ds(al(me_x, blk_i), blk_i)] = out_x[s, slot, :, :, pl.ds(al(me_x, len_j), len_j), :]
-            ty_last[:, :, pl.ds(al(me_y, blk_j), blk_j), :] = out_y[s, slot, :, pl.ds(al(me_y, len_i), len_i)]
+            tx_last[:, pl.ds(al(me_x, blk_i), blk_i)] = out_x[s % banks, slot, :, :, pl.ds(al(me_x, len_j), len_j), :]
+            ty_last[:, :, pl.ds(al(me_y, blk_j), blk_j), :] = out_y[s % banks, slot, :, pl.ds(al(me_y, len_i), len_i)]
         else:
             own_x.start()
             own_y.start()
@@ -222,10 +221,6 @@
         (b3.at[mine, mine], g.at[1, 0]), (b3.at[mine, theirs], g.at[1, 1])))]
     for copy in loads:
         copy.start()
-    size = blk_j * blk_j
-    row = lax.broadcasted_iota(jnp.int32, (size, size), 0)
-    col = lax.broadcasted_iota(jnp.int32, (size, size), 1)
-    perm[...] = jnp.where(col == lax.rem(row, blk_j) * blk_j + row // blk_j, 1.0, 0.0).astype(BF16)
     for copy in loads:
         copy.wait()
     for s in range(2):
@@ -302,6 +297,7 @@
         rhs, len_i, len_j, len_k = x_vol.shape
         m1, m2 = len_i * n1, len_j * n2
         blk_j, blk_i = len_j // n1, len_i // n2
+        banks = 1 if rhs // PER <= SLOTS else 2
         any_spec = pl.BlockSpec(memory_space=pl.ANY)
         vmem_spec = pl.BlockSpec(memory_space=pltpu.VMEM)
         outs = [
@@ -323,17 +319,16 @@
             out_specs=[vmem_spec] * 4 + [any_spec] * (len(outs) - 4),
             scratch_shapes=[
                 vmem((2, m1, m1), BF16), vmem((2, m2, m2), BF16), vmem((2, 2, len_k, len_k), BF16), vmem(local, F32),
-                vmem((blk_j * blk_j, blk_j * blk_j), BF16),
                 vmem((m1, blk_j, len_k), BF16), vmem((blk_i, m2, len_k), BF16),
                 vmem((blk_j, m1, len_k), BF16), vmem((blk_j, m1, len_k), BF16),
-                vmem((2, SLOTS, PER, m1, blk_j, len_k), BF16), vmem((2, SLOTS, PER, blk_i, m2, len_k), BF16),
+                vmem((banks, SLOTS, PER, m1, blk_j, len_k), BF16), vmem((banks, SLOTS, PER, blk_i, m2, len_k), BF16),
                 vmem(local, BF16), vmem(local, BF16), vmem(local, BF16), vmem(local, BF16),
                 vmem(local, BF16),
                 dma((2, rhs // PER, n1 + n2 - 1)), dma((2, rhs // PER, n1 + n2 - 1)),
                 dma((2, rhs // PER, n1 + n2 - 2)), dma((2, rhs // PER, n1 + n2 - 2)),
                 dma((2, SLOTS, 2)), dma((12,)),
             ],
-            compiler_params=pltpu.CompilerParams(collective_id=0, has_side_effects=True, vmem_limit_bytes=45 * 1024 * 1024),
+            compiler_params=pltpu.CompilerParams(collective_id=0, has_side_effects=True, vmem_limit_bytes=42 * 1024 * 1024),
             name='kron',
         )(x_vol, diag_vals, a1, a2, a3, b1, b2, b3)
         return pl.pallas_call(
@@ -342,7 +337,7 @@
             in_specs=[vmem_spec] * 4,
             out_specs=any_spec,
             scratch_shapes=[vmem((PER, *local), F32), dma((rhs,))],
-            compiler_params=pltpu.CompilerParams(vmem_limit_bytes=8 * 1024 * 1024),
+            compiler_params=pltpu.CompilerParams(vmem_limit_bytes=12 * 1024 * 1024),
             name='finish',
         )(*res[:4])
 

time: 376 us -> 375 us (level)
  no operation moved by 1% of the time
where the time goes in v6:
time: 375 us; the launch traced here: 374 us
  Pallas kernels  374 us (100%)
    pallas_call x1, Pallas kernels, local_op(): pl.pallas_call(functools.partial(kernel, n1, n2), out_shape=outs, in_spec...  369 us

profile of v6, /device:TPU:96, one launch (start us, length us, event | category | flops | bytes accessed | tf_op | source)
XLA Modules:
  0.0 374.4 jit_solution(10099429145553194628)
XLA Ops:
  0.0 368.5 %kron.1 = (f32[4,32,64,256]{3,2,1,0:T(8,128)S(1)}, bf16[4,32,64,256]{3,2,1,0:T(8,128)(2,1)S(1)}, bf16[4,32,64,256]{3,2,1,0:T(8,128)(2,1)S(1)}, bf16[4,32,64,256]...) custom-call(bf16[8,32,64,256]{3,2,1,0:T(8,128)(2,1)} %x.1, ...), custom_call_target="tpu_custom_call" | custom-call | tf_op jit(solution)/shard_map/kron/pallas_call | solution.py:315
  368.5 5.9 %finish.1 = f32[8,32,64,256]{3,2,1,0:T(8,128)} custom-call(f32[4,32,64,256]{3,2,1,0:T(8,128)S(1)} %get-tuple-element.9.z_first, bf16[4,32,64,256]{3,2,1,0:T(8,128)(2,1)S(1)} %get-tuple-element.10.third, bf16[4,32,64,256]{3,2,1,0:T(8,128)(2,1)S(1)} %get-tuple-element.11.ty, bf16[4,32,64,256]{3,2,1,0:T(8,128)(2,1)S(1)} %get-tuple-element.12.tx), custom_call_target="tpu_custom_call" | custom-call | tf_op jit(solution)/shard_map/finish/pallas_call | solution.py:334

commit v7 on v6

--- a/solution.py
+++ b/solution.py
@@ -15,7 +15,7 @@
 
 def kernel(n1, n2, x, d, a1, a2, a3, b1, b2, b3, z, third_last, ty_last, tx_last, w, ly, lx, lc, ty, tx,
            f1, f2, g, dv, buf_y, buf_x, mid_a, mid_b, out_y, out_x, vb, cb, yb, xb, ws,
-           in_send, in_recv, out_send, out_recv, own_sem, ld):
+           in_send, in_recv, out_send, out_recv, own_sem, ld, w_sem):
     rhs, len_i, len_j, len_k = x.shape
     blk_j, blk_i = len_j // n1, len_i // n2
     me_y, me_x, me_c = lax.axis_index('mode1'), lax.axis_index('mode2'), lax.axis_index('mode3')
@@ -96,31 +96,43 @@
         for copy in x_list + y_list:
             copy.wait_send()
             copy.wait_recv()
-        blocks = buf_y.shape[0] // blk_j
-
-        def loads_of(t):
+        blocks = buf_y.shape[1] // blk_j
+
+        def loads_of(c):
+            t, half = r * PER + c, lax.rem(c, 2)
             first, second = [], []
             for o in range(n2):
                 p = peer_x(o)
                 src = v.at[t, pl.ds(al(me_x, blk_i), blk_i)] if o == 0 else lx.at[s, t, :, pl.ds(al(p, len_j), len_j), :]
-                first.append(pltpu.make_async_copy(src, buf_x.at[:, pl.ds(al(p, len_j), len_j), :], ld.at[n1 + o]))
+                first.append(pltpu.make_async_copy(src, buf_x.at[half, :, pl.ds(al(p, len_j), len_j), :], ld.at[half, n1 + o]))
             for o in range(n1):
                 q = peer_y(o)
                 src = v.at[t, :, pl.ds(al(me_y, blk_j), blk_j), :] if o == 0 else ly.at[s, t, pl.ds(al(q, len_i), len_i)]
-                second.append(pltpu.make_async_copy(src, buf_y.at[pl.ds(al(q, len_i), len_i)], ld.at[o]))
+                second.append(pltpu.make_async_copy(src, buf_y.at[half, pl.ds(al(q, len_i), len_i)], ld.at[half, o]))
             return first, second
+
+        def start_loads(c):
+            first, second = loads_of(c)
+            for copy in first + second:
+                copy.start()
+
+        start_loads(0)
 
         @pl.loop(0, PER)
         def _(c):
-            first, second = loads_of(r * PER + c)
-            for copy in first + second:
-                copy.start()
+            half = lax.rem(c, 2)
+
+            @pl.when(c + 1 < PER)
+            def _():
+                start_loads(c + 1)
+
+            first, second = loads_of(c)
             for copy in first:
                 copy.wait()
 
             @pl.loop(0, blk_i)
             def _(i):
-                out_x[s % banks, slot, c, i] = jnp.dot(f2[s], buf_x[i], preferred_element_type=F32).astype(BF16)
+                out_x[s % banks, slot, c, i] = jnp.dot(f2[s], buf_x[half, i], preferred_element_type=F32).astype(BF16)
 
             for copy in second:
                 copy.wait()
@@ -128,7 +140,7 @@
             @pl.loop(0, blocks)
             def _(b):
                 rows = pl.ds(al(b, blk_j), blk_j)
-                mid_a[:, rows, :] = jnp.swapaxes(buf_y[rows], 0, 1)
+                mid_a[:, rows, :] = jnp.swapaxes(buf_y[half, rows], 0, 1)
 
             @pl.loop(0, blk_j)
             def _(j):
@@ -170,28 +182,45 @@
             own_x.wait()
             own_y.wait()
 
-    def mode3(s, rows):
-        return (jnp.dot(vb[rows].reshape(flat), g[s, 0], preferred_element_type=F32)
-                + jnp.dot(cb[rows].reshape(flat), g[s, 1], preferred_element_type=F32)).astype(BF16)
+    def mode3(s, half, rows):
+        return (jnp.dot(vb[half, rows].reshape(flat), g[s, 0], preferred_element_type=F32)
+                + jnp.dot(cb[half, rows].reshape(flat), g[s, 1], preferred_element_type=F32)).astype(BF16)
+
+    def store_w(t):
+        return pltpu.make_async_copy(ws, w.at[t], w_sem)
 
     def combine(s, v, r):
         wait_core(s, v, r)
         wait_out(s, r)
 
+        def loads_of(c):
+            t, half = r * PER + c, lax.rem(c, 2)
+            return [pltpu.make_async_copy(src, dst.at[half], ld.at[half, n]) for n, (src, dst) in enumerate(
+                ((v.at[t], vb), (lc.at[s, t], cb), (ty.at[s, t], yb), (tx.at[s, t], xb)))]
+
+        for copy in loads_of(0):
+            copy.start()
+
         @pl.loop(0, PER)
         def _(c):
-            t = r * PER + c
-            loads = [pltpu.make_async_copy(src, dst, ld.at[n]) for n, (src, dst) in enumerate(
-                ((v.at[t], vb), (lc.at[s, t], cb), (ty.at[s, t], yb), (tx.at[s, t], xb)))]
-            for copy in loads:
-                copy.start()
-            for copy in loads:
+            t, half = r * PER + c, lax.rem(c, 2)
+
+            @pl.when(c + 1 < PER)
+            def _():
+                for copy in loads_of(c + 1):
+                    copy.start()
+
+            for copy in loads_of(c):
                 copy.wait()
+            if s == 0:
+                @pl.when(c > 0)
+                def _():
+                    store_w(t - 1).wait()
 
             @pl.loop(0, len_i // step)
             def _(b):
                 rows = pl.ds(b * step, step)
-                total = (yb[rows].reshape(flat).astype(F32) + xb[rows].reshape(flat).astype(F32)) + mode3(s, rows).astype(F32)
+                total = (yb[half, rows].reshape(flat).astype(F32) + xb[half, rows].reshape(flat).astype(F32)) + mode3(s, half, rows).astype(F32)
                 if s == 0:
                     scaled = dv[rows].reshape(flat) * total.astype(BF16).astype(F32)
                     ws[rows] = scaled.astype(BF16).reshape(step, len_j, len_k)
@@ -199,9 +228,10 @@
                     z[t, rows] = total.reshape(step, len_j, len_k)
 
             if s == 0:
-                store = pltpu.make_async_copy(ws, w.at[t], ld.at[0])
-                store.start()
-                store.wait()
+                store_w(t).start()
+
+        if s == 0:
+            store_w(r * PER + PER - 1).wait()
 
     barrier = pltpu.get_barrier_semaphore()
     for o in range(1, n1):
@@ -215,7 +245,7 @@
         send_in(0, x, r)
 
     mine, theirs = pl.ds(al(me_c, len_k), len_k), pl.ds(al(other, len_k), len_k)
-    loads = [pltpu.make_async_copy(src, dst, ld.at[n]) for n, (src, dst) in enumerate((
+    loads = [pltpu.make_async_copy(src, dst, ld.at[0, n]) for n, (src, dst) in enumerate((
         (a1, f1.at[0]), (b1, f1.at[1]), (a2, f2.at[0]), (b2, f2.at[1]), (d, dv),
         (a3.at[mine, mine], g.at[0, 0]), (a3.at[mine, theirs], g.at[0, 1]),
         (b3.at[mine, mine], g.at[1, 0]), (b3.at[mine, theirs], g.at[1, 1])))]
@@ -255,19 +285,29 @@
     combine(1, w, last - 1)
     wait_core(1, w, last)
 
+    def last_loads(c):
+        t, half = last * PER + c, lax.rem(c, 2)
+        return [pltpu.make_async_copy(w.at[t], vb.at[half], ld.at[half, 0]), pltpu.make_async_copy(lc.at[1, t], cb.at[half], ld.at[half, 1])]
+
+    for copy in last_loads(0):
+        copy.start()
+
     @pl.loop(0, PER)
     def _(c):
-        t = last * PER + c
-        loads = [pltpu.make_async_copy(w.at[t], vb, ld.at[0]), pltpu.make_async_copy(lc.at[1, t], cb, ld.at[1])]
-        for copy in loads:
-            copy.start()
-        for copy in loads:
+        half = lax.rem(c, 2)
+
+        @pl.when(c + 1 < PER)
+        def _():
+            for copy in last_loads(c + 1):
+                copy.start()
+
+        for copy in last_loads(c):
             copy.wait()
 
         @pl.loop(0, len_i // step)
         def _(b):
             rows = pl.ds(b * step, step)
-            third_last[c, rows] = mode3(1, rows).reshape(step, len_j, len_k)
+            third_last[c, rows] = mode3(1, half, rows).reshape(step, len_j, len_k)
 
     wait_out(1, last, True)
 
@@ -319,14 +359,14 @@
             out_specs=[vmem_spec] * 4 + [any_spec] * (len(outs) - 4),
             scratch_shapes=[
                 vmem((2, m1, m1), BF16), vmem((2, m2, m2), BF16), vmem((2, 2, len_k, len_k), BF16), vmem(local, F32),
-                vmem((m1, blk_j, len_k), BF16), vmem((blk_i, m2, len_k), BF16),
+                vmem((2, m1, blk_j, len_k), BF16), vmem((2, blk_i, m2, len_k), BF16),
                 vmem((blk_j, m1, len_k), BF16), vmem((blk_j, m1, len_k), BF16),
                 vmem((banks, SLOTS, PER, m1, blk_j, len_k), BF16), vmem((banks, SLOTS, PER, blk_i, m2, len_k), BF16),
-                vmem(local, BF16), vmem(local, BF16), vmem(local, BF16), vmem(local, BF16),
+                *[vmem((2, *local), BF16)] * 4,
                 vmem(local, BF16),
                 dma((2, rhs // PER, n1 + n2 - 1)), dma((2, rhs // PER, n1 + n2 - 1)),
                 dma((2, rhs // PER, n1 + n2 - 2)), dma((2, rhs // PER, n1 + n2 - 2)),
-                dma((2, SLOTS, 2)), dma((12,)),
+                dma((2, SLOTS, 2)), dma((2, 12)), dma,
             ],
             compiler_params=pltpu.CompilerParams(collective_id=0, has_side_effects=True, vmem_limit_bytes=42 * 1024 * 1024),
             name='kron',

time: 375 us -> 375 us (level)
  no operation moved by 1% of the time
where the time goes in v7:
time: 375 us
  Pallas kernels  375 us (100%)
    pallas_call x1, Pallas kernels, local_op(): pl.pallas_call(functools.partial(kernel, n1, n2), out_shape=outs, in_spec...  369 us

profile of v7, /device:TPU:96, one launch (start us, length us, event | category | flops | bytes accessed | tf_op | source)
XLA Modules:
  0.0 374.6 jit_solution(7442222831636016654)
XLA Ops:
  0.0 368.6 %kron.1 = (f32[4,32,64,256]{3,2,1,0:T(8,128)S(1)}, bf16[4,32,64,256]{3,2,1,0:T(8,128)(2,1)S(1)}, bf16[4,32,64,256]{3,2,1,0:T(8,128)(2,1)S(1)}, bf16[4,32,64,256]...) custom-call(bf16[8,32,64,256]{3,2,1,0:T(8,128)(2,1)} %x.1, ...), custom_call_target="tpu_custom_call" | custom-call | tf_op jit(solution)/shard_map/kron/pallas_call | solution.py:355
  368.6 5.9 %finish.1 = f32[8,32,64,256]{3,2,1,0:T(8,128)} custom-call(f32[4,32,64,256]{3,2,1,0:T(8,128)S(1)} %get-tuple-element.9.z_first, bf16[4,32,64,256]{3,2,1,0:T(8,128)(2,1)S(1)} %get-tuple-element.10.third, bf16[4,32,64,256]{3,2,1,0:T(8,128)(2,1)S(1)} %get-tuple-element.11.ty, bf16[4,32,64,256]{3,2,1,0:T(8,128)(2,1)S(1)} %get-tuple-element.12.tx), custom_call_target="tpu_custom_call" | custom-call | tf_op jit(solution)/shard_map/finish/pallas_call | solution.py:374

commit v8 on v7

--- a/solution.py
+++ b/solution.py
@@ -49,12 +49,12 @@
         for o in offsets_y:
             q = peer_y(o)
             y_list.append(remote(v.at[group, :, pl.ds(al(q, blk_j), blk_j), :], ly.at[s, group, pl.ds(al(me_y, len_i), len_i)],
-                                 in_send.at[s, r, o - 1], in_recv.at[s, r, o - 1], 'mode1', q))
+                                 in_send.at[r, 0], in_recv.at[r, 0], 'mode1', q))
         for o in offsets_x:
             p = peer_x(o)
             x_list.append(remote(v.at[group, pl.ds(al(p, blk_i), blk_i)], lx.at[s, group, :, pl.ds(al(me_x, len_j), len_j), :],
-                                 in_send.at[s, r, n1 + o - 2], in_recv.at[s, r, n1 + o - 2], 'mode2', p))
-        core = remote(v.at[group], lc.at[s, group], in_send.at[s, r, n1 + n2 - 2], in_recv.at[s, r, n1 + n2 - 2], 'mode3', other)
+                                 in_send.at[r, 1], in_recv.at[r, 1], 'mode2', p))
+        core = remote(v.at[group], lc.at[s, group], in_send.at[r, 2], in_recv.at[r, 2 + s], 'mode3', other)
         return y_list, x_list, core
 
     def send_in(s, v, r):
@@ -64,17 +64,27 @@
                 copy.start()
         core.start()
 
+    def wait_exchange(send, recv, y_span, x_span, r):
+        for n, (axis, peer, span) in enumerate((('mode1', peer_y(1), y_span), ('mode2', peer_x(1), x_span))):
+            copies = remote(span, span, send.at[r, n], recv.at[r, n], axis, peer)
+            copies.wait_send()
+            copies.wait_recv()
+
+    def wait_in(s, r):
+        group = pl.ds(r * PER, PER)
+        wait_exchange(in_send, in_recv, ly.at[s, group, pl.ds(0, (n1 - 1) * len_i)], lx.at[s, group, :, pl.ds(0, (n2 - 1) * len_j), :], r)
+
     def out_x_copies(s, r, slot, last=False, offsets=all_x):
         copies = []
         home = tx_last if last else tx.at[s, pl.ds(r * PER, PER)]
         for o in offsets:
             p = peer_x(o)
             copies.append(remote(out_x.at[s % banks, slot, :, :, pl.ds(al(p, len_j), len_j), :], home.at[:, pl.ds(al(me_x, blk_i), blk_i)],
-                                 out_send.at[s, r, n1 + o - 2], out_recv.at[s, r, n1 + o - 2], 'mode2', p))
+                                 out_send.at[r, 1], out_recv.at[r, 1], 'mode2', p))
         if last:
             return copies, None
         own = pltpu.make_async_copy(out_x.at[s % banks, slot, :, :, pl.ds(al(me_x, len_j), len_j), :],
-                                    home.at[:, pl.ds(al(me_x, blk_i), blk_i)], own_sem.at[s, slot, 1])
+                                    home.at[:, pl.ds(al(me_x, blk_i), blk_i)], own_sem.at[slot, 1])
         return copies, own
 
     def out_y_copies(s, r, slot, last=False, offsets=all_y):
@@ -83,19 +93,16 @@
         for o in offsets:
             q = peer_y(o)
             copies.append(remote(out_y.at[s % banks, slot, :, pl.ds(al(q, len_i), len_i)], home.at[:, :, pl.ds(al(me_y, blk_j), blk_j), :],
-                                 out_send.at[s, r, o - 1], out_recv.at[s, r, o - 1], 'mode1', q))
+                                 out_send.at[r, 0], out_recv.at[r, 0], 'mode1', q))
         if last:
             return copies, None
         own = pltpu.make_async_copy(out_y.at[s % banks, slot, :, pl.ds(al(me_y, len_i), len_i)],
-                                    home.at[:, :, pl.ds(al(me_y, blk_j), blk_j), :], own_sem.at[s, slot, 0])
+                                    home.at[:, :, pl.ds(al(me_y, blk_j), blk_j), :], own_sem.at[slot, 0])
         return copies, own
 
     def products(s, v, r, last=False):
         slot = lax.rem(r, SLOTS)
-        y_list, x_list, _ = in_copies(s, v, r)
-        for copy in x_list + y_list:
-            copy.wait_send()
-            copy.wait_recv()
+        wait_in(s, r)
         blocks = buf_y.shape[1] // blk_j
 
         def loads_of(c):
@@ -104,11 +111,11 @@
             for o in range(n2):
                 p = peer_x(o)
                 src = v.at[t, pl.ds(al(me_x, blk_i), blk_i)] if o == 0 else lx.at[s, t, :, pl.ds(al(p, len_j), len_j), :]
-                first.append(pltpu.make_async_copy(src, buf_x.at[half, :, pl.ds(al(p, len_j), len_j), :], ld.at[half, n1 + o]))
+                first.append(pltpu.make_async_copy(src, buf_x.at[half, :, pl.ds(al(p, len_j), len_j), :], ld.at[half, 0]))
             for o in range(n1):
                 q = peer_y(o)
                 src = v.at[t, :, pl.ds(al(me_y, blk_j), blk_j), :] if o == 0 else ly.at[s, t, pl.ds(al(q, len_i), len_i)]
-                second.append(pltpu.make_async_copy(src, buf_y.at[half, pl.ds(al(q, len_i), len_i)], ld.at[half, o]))
+                second.append(pltpu.make_async_copy(src, buf_y.at[half, pl.ds(al(q, len_i), len_i)], ld.at[half, 1]))
             return first, second
 
         def start_loads(c):
@@ -126,16 +133,13 @@
             def _():
                 start_loads(c + 1)
 
-            first, second = loads_of(c)
-            for copy in first:
-                copy.wait()
+            pltpu.make_async_copy(buf_x.at[half], buf_x.at[half], ld.at[half, 0]).wait()
 
             @pl.loop(0, blk_i)
             def _(i):
                 out_x[s % banks, slot, c, i] = jnp.dot(f2[s], buf_x[half, i], preferred_element_type=F32).astype(BF16)
 
-            for copy in second:
-                copy.wait()
+            pltpu.make_async_copy(buf_y.at[half], buf_y.at[half], ld.at[half, 1]).wait()
 
             @pl.loop(0, blocks)
             def _(b):
@@ -172,15 +176,13 @@
         core.wait_recv()
 
     def wait_out(s, r, last=False):
-        slot = lax.rem(r, SLOTS)
-        copies_x, own_x = out_x_copies(s, r, slot, last)
-        copies_y, own_y = out_y_copies(s, r, slot, last)
-        for copy in copies_x + copies_y:
-            copy.wait_send()
-            copy.wait_recv()
+        group = pl.ds(0, PER) if last else pl.ds(r * PER, PER)
+        y_home, x_home = (ty_last, tx_last) if last else (ty.at[s], tx.at[s])
+        wait_exchange(out_send, out_recv, y_home.at[group, :, pl.ds(0, (n1 - 1) * blk_j), :], x_home.at[group, pl.ds(0, (n2 - 1) * blk_i)], r)
         if not last:
-            own_x.wait()
-            own_y.wait()
+            slot = lax.rem(r, SLOTS)
+            out_x_copies(s, r, slot)[1].wait()
+            out_y_copies(s, r, slot)[1].wait()
 
     def mode3(s, half, rows):
         return (jnp.dot(vb[half, rows].reshape(flat), g[s, 0], preferred_element_type=F32)
@@ -245,7 +247,7 @@
         send_in(0, x, r)
 
     mine, theirs = pl.ds(al(me_c, len_k), len_k), pl.ds(al(other, len_k), len_k)
-    loads = [pltpu.make_async_copy(src, dst, ld.at[0, n]) for n, (src, dst) in enumerate((
+    loads = [pltpu.make_async_copy(src, dst, w_sem if n == 8 else ld.at[n // 4, n % 4]) for n, (src, dst) in enumerate((
         (a1, f1.at[0]), (b1, f1.at[1]), (a2, f2.at[0]), (b2, f2.at[1]), (d, dv),
         (a3.at[mine, mine], g.at[0, 0]), (a3.at[mine, theirs], g.at[0, 1]),
         (b3.at[mine, mine], g.at[1, 0]), (b3.at[mine, theirs], g.at[1, 1])))]
@@ -314,18 +316,15 @@
 
 def finish(z_first, third, ty, tx, z, zb, sem):
     done, len_i = z_first.shape[0], z_first.shape[1]
-    writes = [pltpu.make_async_copy(z_first.at[r], z.at[r], sem.at[r]) for r in range(done)]
-    for copy in writes:
-        copy.start()
+    for r in range(done):
+        pltpu.make_async_copy(z_first.at[r], z.at[r], sem).start()
     for c in range(third.shape[0]):
         @pl.loop(0, len_i)
         def _(i):
             zb[c, i] = (ty[c, i].astype(F32) + tx[c, i].astype(F32)) + third[c, i].astype(F32)
 
-        writes.append(pltpu.make_async_copy(zb.at[c], z.at[done + c], sem.at[done + c]))
-        writes[-1].start()
-    for copy in writes:
-        copy.wait()
+        pltpu.make_async_copy(zb.at[c], z.at[done + c], sem).start()
+    pltpu.make_async_copy(z, z, sem).wait()
 
 
 def solution(mesh):
@@ -364,9 +363,8 @@
                 vmem((banks, SLOTS, PER, m1, blk_j, len_k), BF16), vmem((banks, SLOTS, PER, blk_i, m2, len_k), BF16),
                 *[vmem((2, *local), BF16)] * 4,
                 vmem(local, BF16),
-                dma((2, rhs // PER, n1 + n2 - 1)), dma((2, rhs // PER, n1 + n2 - 1)),
-                dma((2, rhs // PER, n1 + n2 - 2)), dma((2, rhs // PER, n1 + n2 - 2)),
-                dma((2, SLOTS, 2)), dma((2, 12)), dma,
+                dma((rhs // PER, 3)), dma((rhs // PER, 4)), dma((rhs // PER, 2)), dma((rhs // PER, 2)),
+                dma((SLOTS, 2)), dma((2, 4)), dma,
             ],
             compiler_params=pltpu.CompilerParams(collective_id=0, has_side_effects=True, vmem_limit_bytes=42 * 1024 * 1024),
             name='kron',
@@ -376,7 +374,7 @@
             out_shape=jax.ShapeDtypeStruct(x_vol.shape, F32),
             in_specs=[vmem_spec] * 4,
             out_specs=any_spec,
-            scratch_shapes=[vmem((PER, *local), F32), dma((rhs,))],
+            scratch_shapes=[vmem((PER, *local), F32), dma],
             compiler_params=pltpu.CompilerParams(vmem_limit_bytes=12 * 1024 * 1024),
             name='finish',
         )(*res[:4])

time: 375 us -> 374 us (level)
  no operation moved by 1% of the time
where the time goes in v8:
time: 374 us
  Pallas kernels  374 us (100%)
    pallas_call x1, Pallas kernels, local_op(): pl.pallas_call(functools.partial(kernel, n1, n2), out_shape=outs, in_spec...  368 us

profile of v8, /device:TPU:96, one launch (start us, length us, event | category | flops | bytes accessed | tf_op | source)
XLA Modules:
  0.0 373.6 jit_solution(3558082816379708353)
XLA Ops:
  0.0 367.7 %kron.1 = (f32[4,32,64,256]{3,2,1,0:T(8,128)S(1)}, bf16[4,32,64,256]{3,2,1,0:T(8,128)(2,1)S(1)}, bf16[4,32,64,256]{3,2,1,0:T(8,128)(2,1)S(1)}, bf16[4,32,64,256]...) custom-call(bf16[8,32,64,256]{3,2,1,0:T(8,128)(2,1)} %x.1, ...), custom_call_target="tpu_custom_call" | custom-call | tf_op jit(solution)/shard_map/kron/pallas_call | solution.py:354
  367.7 5.9 %finish.1 = f32[8,32,64,256]{3,2,1,0:T(8,128)} custom-call(f32[4,32,64,256]{3,2,1,0:T(8,128)S(1)} %get-tuple-element.9.z_first, bf16[4,32,64,256]{3,2,1,0:T(8,128)(2,1)S(1)} %get-tuple-element.10.third, bf16[4,32,64,256]{3,2,1,0:T(8,128)(2,1)S(1)} %get-tuple-element.11.ty, bf16[4,32,64,256]{3,2,1,0:T(8,128)(2,1)S(1)} %get-tuple-element.12.tx), custom_call_target="tpu_custom_call" | custom-call | tf_op jit(solution)/shard_map/finish/pallas_call | solution.py:372

commit v9 on v8

--- a/solution.py
+++ b/solution.py
@@ -15,7 +15,7 @@
 
 def kernel(n1, n2, x, d, a1, a2, a3, b1, b2, b3, z, third_last, ty_last, tx_last, w, ly, lx, lc, ty, tx,
            f1, f2, g, dv, buf_y, buf_x, mid_a, mid_b, out_y, out_x, vb, cb, yb, xb, ws,
-           in_send, in_recv, out_send, out_recv, own_sem, ld, w_sem):
+           send_sem, in_recv, out_recv, own_sem, ld, w_sem):
     rhs, len_i, len_j, len_k = x.shape
     blk_j, blk_i = len_j // n1, len_i // n2
     me_y, me_x, me_c = lax.axis_index('mode1'), lax.axis_index('mode2'), lax.axis_index('mode3')
@@ -49,12 +49,12 @@
         for o in offsets_y:
             q = peer_y(o)
             y_list.append(remote(v.at[group, :, pl.ds(al(q, blk_j), blk_j), :], ly.at[s, group, pl.ds(al(me_y, len_i), len_i)],
-                                 in_send.at[r, 0], in_recv.at[r, 0], 'mode1', q))
+                                 send_sem.at[r, 0], in_recv.at[r, 0], 'mode1', q))
         for o in offsets_x:
             p = peer_x(o)
             x_list.append(remote(v.at[group, pl.ds(al(p, blk_i), blk_i)], lx.at[s, group, :, pl.ds(al(me_x, len_j), len_j), :],
-                                 in_send.at[r, 1], in_recv.at[r, 1], 'mode2', p))
-        core = remote(v.at[group], lc.at[s, group], in_send.at[r, 2], in_recv.at[r, 2 + s], 'mode3', other)
+                                 send_sem.at[r, 1], in_recv.at[r, 1], 'mode2', p))
+        core = remote(v.at[group], lc.at[s, group], send_sem.at[r, 2], in_recv.at[r, 2 + s], 'mode3', other)
         return y_list, x_list, core
 
     def send_in(s, v, r):
@@ -72,7 +72,7 @@
 
     def wait_in(s, r):
         group = pl.ds(r * PER, PER)
-        wait_exchange(in_send, in_recv, ly.at[s, group, pl.ds(0, (n1 - 1) * len_i)], lx.at[s, group, :, pl.ds(0, (n2 - 1) * len_j), :], r)
+        wait_exchange(send_sem, in_recv, ly.at[s, group, pl.ds(0, (n1 - 1) * len_i)], lx.at[s, group, :, pl.ds(0, (n2 - 1) * len_j), :], r)
 
     def out_x_copies(s, r, slot, last=False, offsets=all_x):
         copies = []
@@ -80,7 +80,7 @@
         for o in offsets:
             p = peer_x(o)
             copies.append(remote(out_x.at[s % banks, slot, :, :, pl.ds(al(p, len_j), len_j), :], home.at[:, pl.ds(al(me_x, blk_i), blk_i)],
-                                 out_send.at[r, 1], out_recv.at[r, 1], 'mode2', p))
+                                 send_sem.at[r, 1], out_recv.at[r, 1], 'mode2', p))
         if last:
             return copies, None
         own = pltpu.make_async_copy(out_x.at[s % banks, slot, :, :, pl.ds(al(me_x, len_j), len_j), :],
@@ -93,7 +93,7 @@
         for o in offsets:
             q = peer_y(o)
             copies.append(remote(out_y.at[s % banks, slot, :, pl.ds(al(q, len_i), len_i)], home.at[:, :, pl.ds(al(me_y, blk_j), blk_j), :],
-                                 out_send.at[r, 0], out_recv.at[r, 0], 'mode1', q))
+                                 send_sem.at[r, 0], out_recv.at[r, 0], 'mode1', q))
         if last:
             return copies, None
         own = pltpu.make_async_copy(out_y.at[s % banks, slot, :, pl.ds(al(me_y, len_i), len_i)],
@@ -178,7 +178,7 @@
     def wait_out(s, r, last=False):
         group = pl.ds(0, PER) if last else pl.ds(r * PER, PER)
         y_home, x_home = (ty_last, tx_last) if last else (ty.at[s], tx.at[s])
-        wait_exchange(out_send, out_recv, y_home.at[group, :, pl.ds(0, (n1 - 1) * blk_j), :], x_home.at[group, pl.ds(0, (n2 - 1) * blk_i)], r)
+        wait_exchange(send_sem, out_recv, y_home.at[group, :, pl.ds(0, (n1 - 1) * blk_j), :], x_home.at[group, pl.ds(0, (n2 - 1) * blk_i)], r)
         if not last:
             slot = lax.rem(r, SLOTS)
             out_x_copies(s, r, slot)[1].wait()
@@ -363,7 +363,7 @@
                 vmem((banks, SLOTS, PER, m1, blk_j, len_k), BF16), vmem((banks, SLOTS, PER, blk_i, m2, len_k), BF16),
                 *[vmem((2, *local), BF16)] * 4,
                 vmem(local, BF16),
-                dma((rhs // PER, 3)), dma((rhs // PER, 4)), dma((rhs // PER, 2)), dma((rhs // PER, 2)),
+                dma((rhs // PER, 3)), dma((rhs // PER, 4)), dma((rhs // PER, 2)),
                 dma((SLOTS, 2)), dma((2, 4)), dma,
             ],
             compiler_params=pltpu.CompilerParams(collective_id=0, has_side_effects=True, vmem_limit_bytes=42 * 1024 * 1024),

time: 374 us -> 374 us (level)
  no operation moved by 1% of the time
where the time goes in v9:
time: 374 us
  Pallas kernels  374 us (100%)
    pallas_call x1, Pallas kernels, local_op(): pl.pallas_call(functools.partial(kernel, n1, n2), out_shape=outs, in_spec...  368 us

profile of v9, /device:TPU:96, one launch (start us, length us, event | category | flops | bytes accessed | tf_op | source)
XLA Modules:
  0.0 373.5 jit_solution(10873953761083388047)
XLA Ops:
  0.0 367.7 %kron.1 = (f32[4,32,64,256]{3,2,1,0:T(8,128)S(1)}, bf16[4,32,64,256]{3,2,1,0:T(8,128)(2,1)S(1)}, bf16[4,32,64,256]{3,2,1,0:T(8,128)(2,1)S(1)}, bf16[4,32,64,256]...) custom-call(bf16[8,32,64,256]{3,2,1,0:T(8,128)(2,1)} %x.1, ...), custom_call_target="tpu_custom_call" | custom-call | tf_op jit(solution)/shard_map/kron/pallas_call | solution.py:354
  367.7 5.9 %finish.1 = f32[8,32,64,256]{3,2,1,0:T(8,128)} custom-call(f32[4,32,64,256]{3,2,1,0:T(8,128)S(1)} %get-tuple-element.9.z_first, bf16[4,32,64,256]{3,2,1,0:T(8,128)(2,1)S(1)} %get-tuple-element.10.third, bf16[4,32,64,256]{3,2,1,0:T(8,128)(2,1)S(1)} %get-tuple-element.11.ty, bf16[4,32,64,256]{3,2,1,0:T(8,128)(2,1)S(1)} %get-tuple-element.12.tx), custom_call_target="tpu_custom_call" | custom-call | tf_op jit(solution)/shard_map/finish/pallas_call | solution.py:372
